TPU v7x, 256 devices: a whole 4x4x8 slice. The times are simulated.
256 devices in a mesh: member: 8 (over y, core), space: 32 (over z, x).
Axes of the slice: x: 4, y: 4, z: 8, core: 2. Of those that a mesh axis runs over, the one named last changes fastest.
Arguments:
- states: bfloat16 [8, 73, 480, 720], P('member', None, 'space'), may hold values from -6 to 6
- observed: bfloat16 [73, 480, 720], P(None, 'space'), may hold values from -6 to 6
- band_rows: int32 [32], replicated, may hold values from 1 to 15, 361 in all
- encoder_weight: bfloat16 [73, 128], replicated, may hold values from -0.75 to 0.75
- mixing_weight: bfloat16 [128, 128], replicated, may hold values from -0.5 to 0.5
- degree_gain: float32 [368, 128], replicated, may hold values from 0.25 to 2
- decoder_weight: bfloat16 [128, 73], replicated, may hold values from -0.5 to 0.5
Outputs:
- prediction: bfloat16 [8, 73, 480, 720], P('member', None, 'space')
- state_grad: bfloat16 [8, 73, 480, 720], P('member', None, 'space')
Inputs may be any that keep to these rules, and one draw needn't show every extreme that they name: Band d holds the next band_rows[d] latitudes, from the north pole southward, in the first rows of the d-th block of 15 rows; the remaining rows of a block are padding, ignored in states and observed. The bands' rows sum to 361, and some band has exactly 15 rows.
All inputs are finite; a program needn't handle non-finite values.
Results may differ from a plain program's by a relative error of at most 0.014.
Values may be sent and summed in bfloat16 or wider, within the bound.
A program may use at most 128 MiB of HBM per device.

v0:
```python
import math

import jax
import jax.numpy as jnp
from jax import lax
from jax.sharding import PartitionSpec as P

NLAT = 361
LMAX = 360


EPSILON = 1e-05


def grouped_exchange(array, axis, split_dim, concat_dim, work, item_dim, out_dim):

    def moved(group):
        return lax.all_to_all(group, axis, split_axis=split_dim, concat_axis=concat_dim, tiled=True)

    items = jax.tree.leaves(array)[0].shape[item_dim]
    ends = [items * k // 2 for k in range(2 + 1)] if items % 2 == 0 else [0, items]
    groups = [
        jax.tree.map(lambda a: lax.slice_in_dim(a, low, high, axis=item_dim), array)
        for low, high in zip(ends, ends[1:])
    ]
    arrived = [moved(group) for group in groups]
    made = [work(group) for group in arrived]
    return jax.tree.map(lambda *parts: jnp.concatenate(parts, axis=out_dim), *made)


def row_geometry(band_rows, band_len, lat_count):
    band_count = band_rows.shape[0]
    row_index = jnp.arange(band_count * band_len, dtype=jnp.int32)
    row_owner = row_index // band_len
    offset = row_index - row_owner * band_len
    starts = jnp.cumsum(band_rows) - band_rows
    owner_hot = (row_owner[:, None] == jnp.arange(band_count, dtype=jnp.int32)[None, :]).astype(
        jnp.int32
    )
    first_lat = jnp.sum(owner_hot * starts[None, :], axis=1)
    length = jnp.sum(owner_hot * band_rows[None, :], axis=1)
    live_rows = offset < length
    latitude = jnp.minimum(first_lat + offset, lat_count - 1)
    colatitude = latitude.astype(jnp.float32) * (math.pi / (lat_count - 1))
    return (live_rows, jnp.cos(colatitude), jnp.sin(colatitude))


def diagonal_logs(order_count):
    kvalues = jnp.arange(order_count, dtype=jnp.float32)
    increments = jnp.where(
        kvalues >= 1.0, 0.5 * jnp.log((2.0 * kvalues + 1.0) / jnp.maximum(2.0 * kvalues, 1.0)), 0.0
    )
    return 0.5 * math.log(0.5) + jnp.cumsum(increments)


def legendre(orders, log_diag, cosines, sines, top_degree, degrees, quad_weight, live_all):
    order_count = orders.shape[0]
    row_count = cosines.shape[0]
    order_f = orders.astype(jnp.float32)[None, :]
    log_start = (
        log_diag[:, None]
        + orders.astype(jnp.float32)[:, None] * jnp.log(jnp.maximum(sines, 1e-30))[None, :]
    )
    empty_rows = jnp.zeros((order_count, row_count), jnp.float32)
    cosine_row = cosines[None, :]
    degree_int = jnp.arange(degrees, dtype=jnp.int32)
    degree_f = degree_int.astype(jnp.float32)[:, None]
    up_table = jnp.sqrt(
        (4.0 * degree_f * degree_f - 1.0)
        / jnp.maximum(degree_f * degree_f - order_f * order_f, 1.0)
    )
    back_table = jnp.sqrt(
        jnp.maximum((degree_f - 1.0) * (degree_f - 1.0) - order_f * order_f, 0.0)
        / jnp.maximum(4.0 * (degree_f - 1.0) * (degree_f - 1.0) - 1.0, 1.0)
    )
    past_table = degree_int[:, None] > orders[None, :]
    onset_table = degree_int[:, None] == orders[None, :]
    keep_table = (past_table | onset_table) & (degree_int[:, None] <= top_degree)
    block_count = degrees // 16
    quad_row = quad_weight[None, None, :]
    live_row = live_all[None, None, :]

    def blocked(table):
        return table.reshape((block_count, 16) + table.shape[1:])

    def recur_block(state_in, inputs):
        first, second, log_scale = state_in
        up_block, back_block, past_block, onset_block, keep_block = inputs
        stacked = []
        for position in range(16):
            current = jnp.where(
                past_block[position][:, None],
                up_block[position][:, None]
                * (cosine_row * first - back_block[position][:, None] * second),
                jnp.where(onset_block[position][:, None], 1.0, 0.0),
            )
            stacked.append(current)
            second = first
            first = current
        values = jnp.stack(stacked) * jnp.exp(log_scale)[None]
        values = jnp.where(keep_block[:, :, None], values, 0.0)
        forward_part = (values * quad_row).astype(jnp.bfloat16)
        inverse_part = (values * live_row).astype(jnp.bfloat16)
        magnitude = jnp.maximum(jnp.abs(first), jnp.abs(second))
        factor = jnp.where(magnitude > 1.0, magnitude, 1.0)
        return (
            (first / factor, second / factor, log_scale + jnp.log(factor)),
            (forward_part, inverse_part),
        )

    scanned = (
        blocked(up_table),
        blocked(back_table),
        blocked(past_table),
        blocked(onset_table),
        blocked(keep_table),
    )
    final_state, tables = lax.scan(recur_block, (empty_rows, empty_rows, log_start), scanned)
    forward_table = tables[0].reshape(degrees, order_count, row_count)
    inverse_table = tables[1].reshape(degrees, order_count, row_count)
    return (forward_table, inverse_table)


def transforms(lon_count, order_count, top_degree):
    lon_index = jnp.arange(lon_count, dtype=jnp.int32)
    order_index = jnp.arange(order_count, dtype=jnp.int32)
    angle_table = (order_index[:, None] * lon_index[None, :] % lon_count).astype(jnp.float32) * (
        2.0 * math.pi / lon_count
    )
    live_order = (order_index <= top_degree)[:, None]
    cosines = jnp.where(live_order, jnp.cos(angle_table), 0.0)
    sines = jnp.where(live_order, jnp.sin(angle_table), 0.0)
    weight = jnp.where((order_index == 0) | (2 * order_index == lon_count), 1.0, 2.0)[:, None]
    forward = jnp.transpose(jnp.stack([cosines, -sines]), (2, 0, 1)) / lon_count
    inverse = jnp.stack([weight * cosines, -weight * sines])
    return (forward.astype(jnp.bfloat16), inverse.astype(jnp.bfloat16))


def gelu_slope(values):
    return 0.5 * (1.0 + lax.erf(values * (1.0 / math.sqrt(2.0)))) + values * jnp.exp(
        -0.5 * values * values
    ) * (1.0 / math.sqrt(2.0 * math.pi))


def score_block(own_fields, everyone, observed, area_weight):
    own_f = own_fields.astype(jnp.float32)
    truth_gap = own_f - observed.astype(jnp.float32)[None]
    truth_dist = jnp.sqrt(jnp.sum(truth_gap * truth_gap, axis=1, keepdims=True) + EPSILON)

    def accumulate(running, other_member):
        member_gap = own_f - other_member.astype(jnp.float32)[None]
        member_dist = jnp.sqrt(jnp.sum(member_gap * member_gap, axis=1, keepdims=True) + EPSILON)
        return (running + member_gap / member_dist, None)

    pair_sum, unused = lax.scan(accumulate, jnp.zeros(own_f.shape, jnp.float32), everyone)
    result = area_weight[None, None, :, None] * (
        truth_gap / truth_dist - pair_sum / everyone.shape[0]
    )
    return result.astype(jnp.bfloat16)


def to_orders(block, finish):
    return grouped_exchange(block, "space", 1, 2, finish, 3, 3)


def to_bands(block, finish):
    return finish(lax.all_to_all(block, "space", split_axis=2, concat_axis=1, tiled=True))


def on_device(
    states, observed, band_rows, encoder_weight, mixing_weight, degree_gain, decoder_weight
):
    space_size = lax.axis_size("space")
    space_index = lax.axis_index("space")
    band_len = states.shape[2]
    lon_count = states.shape[3]
    order_dev = LMAX // space_size + 1
    order_count = order_dev * space_size
    degrees = degree_gain.shape[0]
    live_rows, cosines, sines = row_geometry(band_rows, band_len, NLAT)
    live_all = live_rows.astype(jnp.float32)
    first_order = space_index * order_dev
    orders = first_order + jnp.arange(order_dev, dtype=jnp.int32)
    log_diag = lax.dynamic_slice_in_dim(diagonal_logs(order_count), first_order, order_dev)
    quad_weight = live_all * sines * (math.pi / (NLAT - 1))
    legendre_forward, legendre_inverse = legendre(
        orders, log_diag, cosines, sines, LMAX, degrees, quad_weight, live_all
    )
    fwd_table, inv_table = transforms(lon_count, order_count, LMAX)
    live_own = lax.dynamic_slice_in_dim(live_all, space_index * band_len, band_len)
    sines_own = lax.dynamic_slice_in_dim(sines, space_index * band_len, band_len)
    area_weight = 8.0 * sines_own * live_own
    member = states[0]
    hidden = (
        jnp.einsum("frl,fc->rlc", member, encoder_weight, preferred_element_type=jnp.float32)
        * live_own[:, None, None]
    ).astype(jnp.bfloat16)
    longitude_modes = jnp.einsum(
        "rlc,lkm->kmrc", hidden, fwd_table, preferred_element_type=jnp.float32
    ).astype(jnp.bfloat16)

    def analyse(incoming_rows):
        return jnp.einsum(
            "ghqn,uhq->guhn", incoming_rows, legendre_forward, preferred_element_type=jnp.float32
        ).astype(jnp.bfloat16)

    harmonic_weights = to_orders(longitude_modes, analyse)
    masked_spectrum = (
        jnp.einsum(
            "klmc,cd->klmd", harmonic_weights, mixing_weight, preferred_element_type=jnp.float32
        )
        * degree_gain[None, :, None, :]
    ).astype(jnp.bfloat16)
    rebuilt_field = jnp.einsum(
        "pjcx,jco->pcox", masked_spectrum, legendre_inverse, preferred_element_type=jnp.float32
    ).astype(jnp.bfloat16)

    def longitudes(incoming_rows):
        return jnp.einsum(
            "kmrc,kml->rlc", incoming_rows, inv_table, preferred_element_type=jnp.float32
        )

    grid_field = to_bands(rebuilt_field, longitudes)
    block_out = (
        (jax.nn.gelu(grid_field, approximate=False) + hidden.astype(jnp.float32))
        * live_own[:, None, None]
    ).astype(jnp.bfloat16)
    decoded = jnp.einsum(
        "rlc,cf->frl", block_out, decoder_weight, preferred_element_type=jnp.float32
    )
    prediction = ((member.astype(jnp.float32) + decoded) * live_own[None, :, None]).astype(
        jnp.bfloat16
    )[None]
    lon_share = lon_count // lax.axis_size("member")
    regrouped = lax.all_to_all(prediction, "member", split_axis=3, concat_axis=0, tiled=True)
    truth_share = lax.dynamic_slice_in_dim(
        observed, lax.axis_index("member") * lon_share, lon_share, 2
    )
    score_share = score_block(regrouped, regrouped, truth_share, area_weight)
    score_grad = lax.all_to_all(score_share, "member", split_axis=0, concat_axis=3, tiled=True)
    grad_pred = score_grad[0]
    grad_block = jnp.einsum(
        "frl,cf->rlc", grad_pred, decoder_weight, preferred_element_type=jnp.float32
    )
    grad_field = (grad_block * gelu_slope(grid_field)).astype(jnp.bfloat16)
    rebuilt_gradient = jnp.einsum(
        "rlc,kml->kmrc", grad_field, inv_table, preferred_element_type=jnp.float32
    ).astype(jnp.bfloat16)

    def project(incoming_rows):
        return jnp.einsum(
            "ghqn,uhq->guhn", incoming_rows, legendre_inverse, preferred_element_type=jnp.float32
        )

    masked_gradient = to_orders(rebuilt_gradient, project)
    grad_scaled = (masked_gradient * degree_gain[None, :, None, :]).astype(jnp.bfloat16)
    harmonic_gradient = jnp.einsum(
        "klmd,cd->klmc", grad_scaled, mixing_weight, preferred_element_type=jnp.float32
    ).astype(jnp.bfloat16)
    longitude_gradient = jnp.einsum(
        "sbzv,bze->szev", harmonic_gradient, legendre_forward, preferred_element_type=jnp.float32
    ).astype(jnp.bfloat16)

    def spread(incoming_rows):
        return jnp.einsum(
            "kmrc,lkm->rlc", incoming_rows, fwd_table, preferred_element_type=jnp.float32
        )

    grad_spectral = to_bands(longitude_gradient, spread)
    grad_hidden = ((grad_block + grad_spectral) * live_own[:, None, None]).astype(jnp.bfloat16)
    encoded_back = jnp.einsum(
        "rlc,fc->frl", grad_hidden, encoder_weight, preferred_element_type=jnp.float32
    )
    state_grad = ((grad_pred.astype(jnp.float32) + encoded_back) * live_own[None, :, None]).astype(
        jnp.bfloat16
    )[None]
    return (prediction, state_grad)


def solution(mesh):
    in_specs = (P("member", None, "space", None), P(None, "space", None), P(), P(), P(), P(), P())
    out_specs = (P("member", None, "space", None), P("member", None, "space", None))
    return jax.shard_map(
        on_device, mesh=mesh, in_specs=in_specs, out_specs=out_specs, check_vma=False
    )
```

profile of v0, /device:TPU:7, one launch (start us, length us, event | category | flops | bytes accessed | tf_op | source)
XLA Modules:
  0.0 693.2 jit_solution(13400938999284185063)
XLA Ops:
  3.2 3.3 multiply_convert_fusion.2
  6.5 5.7 multiply_convert_fusion.8
  16.7 5.8 copy.137
  22.6 2.9 reshape.1318
  25.5 11.0 %all-to-all-start.1 = ((bf16[32,2,11520]{2,1,0:T(2,128)(2,1)}), bf16[32,2,11520]{2,1,0:T(2,128)(2,1)}, u32[]{:S(2)}, u32[]{:S(2)}) async-start(bf16[32,2,11520]{2,1,0:T(2,128)(2,1)} %reshape.1318), calls=%async_computation.1 | async-start | bytes 2949120 | tf_op jit(solution)/shard_map/all_to_all | solution.py:18
  37.0 5.8 copy.133
  42.9 2.9 reshape.1320
  46.8 26.6 %all-to-all-done.1 = bf16[32,2,11520]{2,1,0:T(2,128)(2,1)} async-done(((bf16[32,2,11520]{2,1,0:T(2,128)(2,1)}), bf16[32,2,11520]{2,1,0:T(2,128)(2,1)}, u32[]{:S(2)}, u32[]{:S(2)}) %all-to-all-start.1) | async-done | bytes 1474592 | tf_op jit(solution)/shard_map/all_to_all | solution.py:18
  73.4 5.2 all-to-all-start
  78.6 65.8 %while.30 = (s32[]{:T(128)}, f32[12,480]{1,0:T(8,128)S(1)}, f32[12,480]{1,0:T(8,128)S(1)}, f32[12,480]{1,0:T(8,128)S(1)}, bf16[23,16,12,480]{3,2,1,0:T(8,128)(2,...) while((s32[]{:T(128)}, f32[12,480]{1,0:T(8,128)S(1)}, ...), condition=%wide.region_6.7_spmd.clone, body=%wide.region_5.6_spmd.clone.sunk | while | flops 1664849 | bytes 3135831 | solution.py:118
  144.5 8.7 %copy.177 = bf16[368,12,480,1]{0,2,3,1:T(8,128)(2,1)} copy(bf16[368,12,480,1]{2,1,0,3:T(8,128)(2,1)} %bitcast.474) | data formatting | bytes 8478720 | tf_op jit(solution)/shard_map/reshape | solution.py:120
  153.2 8.7 %copy.174 = bf16[368,12,480,1]{0,2,3,1:T(8,128)(2,1)} copy(bf16[368,12,480,1]{2,1,0,3:T(8,128)(2,1)} %bitcast.473) | data formatting | bytes 8478720 | tf_op jit(solution)/shard_map/reshape | solution.py:119
  161.9 3.5 reshape.1319
  165.4 4.2 copy.138
  169.6 3.5 reshape.1321
  175.7 4.6 fusion.203
  182.5 6.0 convert_bitcast_fusion.1
  190.8 75.6 %all_to_all.141 = bf16[2,12,480,128]{3,0,1,2:T(2,128)(2,1)S(1)} all-to-all(bf16[2,12,480,128]{3,0,1,2:T(2,128)(2,1)S(1)} %copy.143), channel_id=1, replica_groups=mesh['member'=8,'space'=32] {'space'}, dimensions={2} | all-to-all | bytes 5898240 | tf_op jit(solution)/shard_map/all_to_all | solution.py:167
  273.4 13.6 %fusion.187 = bf16[1,73,15,720]{3,1,2,0:T(8,128)(2,1)S(1)} fusion(f32[15]{0:T(128)S(1)} %get-tuple-element.241, bf16[1,73,15,720]{3,2,1,0:T(8,128)(2,1)S(1)} %copy-done.8, f32[720,15,128,1]{2,0,3,1:T(8,128)S(1)} %fusion.129, bf16[15,720,128]{2,1,0:T(8,128)(2,1)S(1)} %copy-done.7, bf16[128,73]{0,1:T(8,128)(2,1)S(1)} %copy-done.17), kind=kOutput, calls=%fused_computation.286 | convolution fusion | flops 298987264 | bytes 11466748 | tf_op jit(solution)/shard_map/rlc,cf->frl/dot_general | solution.py:228
  287.0 3.9 copy.147
  291.0 8.6 %all-to-all-start.3 = ((bf16[1,73,15,720]{1,2,0,3:T(8,128)(2,1)}), bf16[1,73,15,720]{1,2,0,3:T(8,128)(2,1)S(1)}, u32[]{:S(2)}, u32[]{:S(2)}) async-start(bf16[1,73,15,720]{1,2,0,3:T(8,128)(2,1)} %copy.147), calls=%async_computation.3 | async-start | bytes 5898240 | tf_op jit(solution)/shard_map/all_to_all | solution.py:235
  301.6 33.2 %all-to-all-done.3 = bf16[1,73,15,720]{1,2,0,3:T(8,128)(2,1)S(1)} async-done(((bf16[1,73,15,720]{1,2,0,3:T(8,128)(2,1)}), bf16[1,73,15,720]{1,2,0,3:T(8,128)(2,1)S(1)}, u32[]{:S(2)}, u32[]{:S(2)}) %all-to-all-start.3) | async-done | bytes 1576832 | tf_op jit(solution)/shard_map/all_to_all | solution.py:235
  334.8 4.8 copy.149
  339.6 6.5 copy.193
  346.4 3.1 copy.150
  349.5 85.1 %while.31 = (s32[]{:T(128)}, f32[8,73,15,90]{3,2,1,0:T(8,128)}, bf16[8,73,15,90]{3,2,1,0:T(8,128)(2,1)}, f32[8,73,15,90]{3,2,1,0:T(8,128)}, s32[]{:T(128)}, /*index=5*/s32[]{:T(128)}) while((s32[]{:T(128)}, f32[8,73,15,90]{3,2,1,0:T(8,128)}, bf16[8,73,15,90]{3,2,1,0:T(8,128)(2,1)}, f32[8,73,15,90]{3,2,1,0:T(8,128)}, s32[]{:T(128)}, ...), condition=%wide.region_10.11_spmd.clone, body=%wide.region_8.10_spmd.clone.sunk | while | flops 5617353 | bytes 14166991 | solution.py:155
  350.6 3.1 multiply_reduce_fusion.3
  353.7 5.3 select_add_fusion.2
  359.9 3.1 multiply_reduce_fusion.3
  363.0 6.7 select_add_fusion.2
  370.8 3.1 multiply_reduce_fusion.3
  373.9 6.7 select_add_fusion.2
  381.6 3.1 multiply_reduce_fusion.3
  384.7 6.7 select_add_fusion.2
  392.4 3.1 multiply_reduce_fusion.3
  395.5 6.7 select_add_fusion.2
  403.2 3.1 multiply_reduce_fusion.3
  406.3 6.7 select_add_fusion.2
  414.0 3.1 multiply_reduce_fusion.3
  417.1 6.7 select_add_fusion.2
  424.8 3.1 multiply_reduce_fusion.3
  427.9 6.7 select_add_fusion.2
  435.5 5.1 fusion.118
  441.0 33.4 %all_to_all.142 = bf16[8,73,15,90]{3,2,1,0:T(8,128)(2,1)S(1)} all-to-all(bf16[8,73,15,90]{3,2,1,0:T(8,128)(2,1)S(1)} %copy.152), channel_id=1, replica_groups=mesh['member'=8,'space'=32] {'member'}, dimensions={0} | all-to-all | bytes 3153600 | tf_op jit(solution)/shard_map/all_to_all | solution.py:240
  474.9 3.2 reshape.1315
  478.1 3.2 fusion.227
  481.4 8.2 %fusion.180 = bf16[2,384,15,128]{1,3,2,0:T(8,128)(2,1)S(1)} fusion(f32[15,720,128]{2,1,0:T(8,128)S(1)} %fusion.227, f32[720,15,128,1]{2,0,3,1:T(8,128)} %copy-done.20, bf16[1,384,720]{1,2,0:T(8,128)(2,1)S(1)} %copy-done.14, bf16[1,384,720]{1,2,0:T(8,128)(2,1)S(1)} %copy-done.12), kind=kOutput, calls=%fused_computation.285 | convolution fusion | flops 2140876800 | bytes 15114240 | tf_op jit(solution)/shard_map/rlc,kml->kmrc/dot_general | solution.py:246
  491.6 5.8 copy.161
  500.3 5.0 all-to-all-start.6
  505.4 5.8 copy.156
  514.1 28.2 %all-to-all-done.6 = bf16[32,2,11520]{2,1,0:T(2,128)(2,1)} async-done(((bf16[32,2,11520]{2,1,0:T(2,128)(2,1)}), bf16[32,2,11520]{2,1,0:T(2,128)(2,1)}, u32[]{:S(2)}, u32[]{:S(2)}) %all-to-all-start.6) | async-done | bytes 1474592 | tf_op jit(solution)/shard_map/all_to_all | solution.py:18
  542.4 4.7 all-to-all-start.5
  547.1 3.5 reshape.1323
  553.2 6.0 fusion.167
  559.2 23.5 %all-to-all-done.5 = bf16[32,2,11520]{2,1,0:T(2,128)(2,1)} async-done(((bf16[32,2,11520]{2,1,0:T(2,128)(2,1)}), bf16[32,2,11520]{2,1,0:T(2,128)(2,1)}, u32[]{:S(2)}, u32[]{:S(2)}) %all-to-all-start.5) | async-done | bytes 1474592 | tf_op jit(solution)/shard_map/all_to_all | solution.py:18
  582.7 3.7 reshape.1325
  589.0 6.0 fusion.164
  595.0 7.4 %convert_bitcast_fusion = bf16[2,12,480,128]{3,2,0,1:T(8,128)(2,1)S(1)} fusion(bf16[368,12,480,1]{0,2,3,1:T(8,128)(2,1)} %copy.174, f32[2,368,12,64]{3,1,0,2:T(8,128)} %fusion.167, f32[2,368,12,64]{3,1,0,2:T(8,128)} %fusion.164, f32[368,128]{1,0:T(8,128)S(1)} %copy-done.16, bf16[128,128]{1,0:T(8,128)(2,1)S(1)} %copy-done), kind=kOutput, calls=%fused_computation.260 | convolution fusion | flops 1380679680 | bytes 11931648 | tf_op jit(solution)/shard_map/sbzv,bze->szev/dot_general | solution.py:260
  602.4 3.8 copy.167
  606.2 6.0 all-to-all-start.7
  612.2 3.3 copy.171
  615.5 63.9 %all-to-all-done.7 = bf16[2,12,480,128]{3,0,1,2:T(2,128)(2,1)S(1)} async-done(((bf16[2,12,480,128]{3,0,1,2:T(2,128)(2,1)}), bf16[2,12,480,128]{3,0,1,2:T(2,128)(2,1)S(1)}, u32[]{:S(2)}, u32[]{:S(2)}) %all-to-all-start.7) | async-done | bytes 2949152 | tf_op jit(solution)/shard_map/all_to_all | solution.py:167
  679.4 3.6 copy.169
  683.0 8.1 %fusion.188 = bf16[1,73,15,720]{3,1,2,0:T(8,128)(2,1)S(1)} fusion(bf16[73,15,720]{2,0,1:T(8,128)(2,1)} %reshape.1315, f32[15]{0:T(128)S(1)} %get-tuple-element.241, f32[15,720,128]{2,1,0:T(8,128)} %copy-done.3, bf16[2,384,15,128]{3,0,2,1:T(2,128)(2,1)} %bitcast.476, f32[1,384,720]{1,2,0:T(8,128)} %copy-done.9, f32[1,384,720]{1,2,0:T(8,128)} %copy-done.10, ...), kind=kOutput, calls=%fused_computation.287 | convolution fusion | flops 2334156800 | bytes 13862908 | tf_op jit(solution)/shard_map/rlc,fc->frl/dot_general | solution.py:271
  (624 shorter events, 112.6 us)
Async XLA Ops:
  0.6 181.9 %copy-start = (bf16[128,128]{1,0:T(8,128)(2,1)S(1)}, bf16[128,128]{1,0:T(8,128)(2,1)}, u32[]{:S(2)}) copy-start(bf16[128,128]{1,0:T(8,128)(2,1)} %param.15) | copy-start | bytes 98308
  6.5 8.3 %copy-start.6 = (bf16[15,720,128]{2,1,0:T(8,128)(2,1)}, bf16[15,720,128]{2,1,0:T(8,128)(2,1)S(1)}, u32[]{:S(2)}) copy-start(bf16[15,720,128]{2,1,0:T(8,128)(2,1)S(1)} %multiply_convert_fusion.2) | copy-start | bytes 8294404
  12.2 2.6 copy-start.9
  12.2 2.6 copy-start.10
  25.5 47.9 %all-to-all-start.1 = ((bf16[32,2,11520]{2,1,0:T(2,128)(2,1)}), bf16[32,2,11520]{2,1,0:T(2,128)(2,1)}, u32[]{:S(2)}, u32[]{:S(2)}) async-start(bf16[32,2,11520]{2,1,0:T(2,128)(2,1)} %reshape.1318), calls=%async_computation.1 | async-start | bytes 2949120 | tf_op jit(solution)/shard_map/all_to_all | solution.py:18
  73.4 96.2 %all-to-all-start = ((bf16[32,2,11520]{2,1,0:T(2,128)(2,1)}), bf16[32,2,11520]{2,1,0:T(2,128)(2,1)}, u32[]{:S(2)}, u32[]{:S(2)}) async-start(bf16[32,2,11520]{2,1,0:T(2,128)(2,1)} %reshape.1320), calls=%async_computation | async-start | bytes 2949120 | tf_op jit(solution)/shard_map/all_to_all | solution.py:18
  173.1 2.6 copy-start.5
  175.7 4.6 slice-start
  175.7 4.6 slice-start.1
  180.3 2.2 copy-start.15
  266.4 2.0 copy-start.11
  266.4 2.0 copy-start.13
  268.5 4.9 copy-start.7
  268.5 4.9 copy-start.8
  268.5 4.9 copy-start.17
  271.0 2.4 copy-start.20
  287.0 3.9 copy-start.2
  291.0 43.9 %all-to-all-start.3 = ((bf16[1,73,15,720]{1,2,0,3:T(8,128)(2,1)}), bf16[1,73,15,720]{1,2,0,3:T(8,128)(2,1)S(1)}, u32[]{:S(2)}, u32[]{:S(2)}) async-start(bf16[1,73,15,720]{1,2,0,3:T(8,128)(2,1)} %copy.147), calls=%async_computation.3 | async-start | bytes 5898240 | tf_op jit(solution)/shard_map/all_to_all | solution.py:235
  334.8 4.8 copy-start.1
  349.5 85.1 %copy-start.4 = (f32[73,15,90]{2,1,0:T(8,128)S(1)}, f32[73,15,90]{2,1,0:T(8,128)}, u32[]{:S(2)}) copy-start(f32[73,15,90]{2,1,0:T(8,128)} %dynamic-slice_convert_fusion) | copy-start | bytes 1182604
  474.3 3.8 copy-start.18
  478.1 3.2 copy-start.12
  478.1 3.2 copy-start.14
  481.4 8.2 %copy-start.3 = (f32[15,720,128]{2,1,0:T(8,128)}, f32[15,720,128]{2,1,0:T(8,128)S(1)}, u32[]{:S(2)}) copy-start(f32[15,720,128]{2,1,0:T(8,128)S(1)} %fusion.227) | copy-start | bytes 16588804
  500.3 42.1 %all-to-all-start.6 = ((bf16[32,2,11520]{2,1,0:T(2,128)(2,1)}), bf16[32,2,11520]{2,1,0:T(2,128)(2,1)}, u32[]{:S(2)}, u32[]{:S(2)}) async-start(bf16[32,2,11520]{2,1,0:T(2,128)(2,1)} %reshape.1322), calls=%async_computation.6 | async-start | bytes 2949120 | tf_op jit(solution)/shard_map/all_to_all | solution.py:18
  542.4 40.3 %all-to-all-start.5 = ((bf16[32,2,11520]{2,1,0:T(2,128)(2,1)}), bf16[32,2,11520]{2,1,0:T(2,128)(2,1)}, u32[]{:S(2)}, u32[]{:S(2)}) async-start(bf16[32,2,11520]{2,1,0:T(2,128)(2,1)} %reshape.1324), calls=%async_computation.5 | async-start | bytes 2949120 | tf_op jit(solution)/shard_map/all_to_all | solution.py:18
  589.0 6.0 copy-start.16
  606.2 73.1 %all-to-all-start.7 = ((bf16[2,12,480,128]{3,0,1,2:T(2,128)(2,1)}), bf16[2,12,480,128]{3,0,1,2:T(2,128)(2,1)S(1)}, u32[]{:S(2)}, u32[]{:S(2)}) async-start(bf16[2,12,480,128]{3,0,1,2:T(2,128)(2,1)} %copy.167), calls=%async_computation.7 | async-start | bytes 5898240 | tf_op jit(solution)/shard_map/all_to_all | solution.py:167
  612.2 70.8 %copy-start.19 = (bf16[73,128]{1,0:T(8,128)(2,1)S(1)}, bf16[73,128]{1,0:T(8,128)(2,1)}, u32[]{:S(2)}) copy-start(bf16[73,128]{1,0:T(8,128)(2,1)} %param.14) | copy-start | bytes 56068
where the time goes:
time: 704 us; the launch traced here: 693 us
  waiting for transfers between devices  175 us (25%)
  other arithmetic  161 us (23%)
  local copies, waits for them, and re-layouts  129 us (18%)
  blocking collectives  109 us (15%)
  matrix products  73.6 us (10%)
  starting transfers between devices  40.6 us (6%)
    all_to_all x4, waiting for transfers between devices, moved(): lax.all_to_all(group, axis, split_axis=split_dim, concat_axis=concat_dim,...  78.4 us
    all_to_all x1, blocking collectives, to_bands(): lax.all_to_all(block, 'space', split_axis=2, concat_axis=1, tiled=True)  75.6 us
    all_to_all x1, waiting for transfers between devices, to_bands(): lax.all_to_all(block, 'space', split_axis=2, concat_axis=1, tiled=True)  63.9 us
    add x8, other arithmetic, accumulate(): return (running + member_gap / member_dist, None)  52.2 us
    unnamed x58, local copies, waits for them, and re-layouts  41.3 us
    all_to_all x1, blocking collectives, on_device(): lax.all_to_all(score_share, 'member', split_axis=0, concat_axis=3, tiled=...  33.4 us
    all_to_all x1, waiting for transfers between devices, on_device(): lax.all_to_all(prediction, 'member', split_axis=3, concat_axis=0, tiled=T...  33.2 us
    while x345, other arithmetic  31.4 us
  transfers between devices with their start and end apart: 6, of which 5 were waited for; matrix products, arithmetic and copies ran while one was open for 18% of the time, Pallas kernels for 0%

commit v1 on v0

v1 whole, which is shorter than its diff:
```python
import functools
import math

import jax
import jax.numpy as jnp
import numpy as np
from jax import lax
from jax.experimental import pallas as pl
from jax.experimental.pallas import tpu as pltpu
from jax.sharding import PartitionSpec as P

NLAT = 361
LMAX = 360
NLON = 720
FIELDS = 73
CH = 128
BAND = 15
BANDS = 32
MEMBERS = 8
MDEV = 12
DEG = 384
PTS = 512
KM = 2 * MDEV
FLAT = 1152
WIDE = BAND * CH

EPSILON = 1e-05
F32 = jnp.float32
BF16 = jnp.bfloat16


def dot(a, b, ca, cb):
    return lax.dot_general(a, b, (((ca,), (cb,)), ((), ())), preferred_element_type=F32)


def params(mb=56):
    return pltpu.CompilerParams(
        vmem_limit_bytes=mb * 1024 * 1024, dimension_semantics=("arbitrary",)
    )


def whole(shape):
    return pl.BlockSpec(shape, lambda *g: (0,) * len(shape))


SMEM = pl.BlockSpec(memory_space=pltpu.SMEM)


def fourier_table():
    orders = np.arange(BANDS * MDEV)
    angle = 2.0 * np.pi * ((orders[:, None] * np.arange(NLON)[None, :]) % NLON) / NLON
    live = (orders <= LMAX)[:, None]
    both = np.stack([np.where(live, np.cos(angle), 0.0), np.where(live, -np.sin(angle), 0.0)])
    both = both.reshape(2, BANDS, MDEV, NLON).transpose(1, 0, 2, 3).reshape(BANDS * KM, NLON)
    return jnp.asarray(both.astype(np.float32), BF16)


def diagonal_logs():
    k = np.arange(1, BANDS * MDEV + 16, dtype=np.float64)
    steps = 0.5 * np.log((2.0 * k + 1.0) / (2.0 * k))
    return np.concatenate([[0.0], np.cumsum(steps)]).astype(np.float32) + np.float32(
        0.5 * math.log(0.5)
    )


def legendre_kernel(first_ref, geo_ref, diag_ref, leg_ref, legt_ref, table):
    step = pl.program_id(0)

    @pl.when(step == 0)
    def _():
        first_order = first_ref[0]
        cosine = jnp.broadcast_to(geo_ref[0:1, :], (16, PTS))
        log_sine = geo_ref[1:2, :]
        live = jnp.broadcast_to(geo_ref[2:3, :], (16, PTS))
        orders = first_order + lax.broadcasted_iota(jnp.int32, (16, 128), 0)
        order_f = orders.astype(F32)
        order_sq = order_f * order_f

        def wide(x):
            return jnp.concatenate([x] * (PTS // 128), axis=1)

        start = wide(diag_ref[...]) + wide(order_f) * log_sine

        def block(number, carry):
            first, second, log_scale = carry
            scale = jnp.exp(log_scale) * live
            for position in range(16):
                degree = number * 16 + position
                lf = jnp.full((16, 128), degree, jnp.int32).astype(F32)
                up = jnp.sqrt((4.0 * lf * lf - 1.0) / jnp.maximum(lf * lf - order_sq, 1.0))
                lb = lf - 1.0
                back = jnp.sqrt(
                    jnp.maximum(lb * lb - order_sq, 0.0) / jnp.maximum(4.0 * lb * lb - 1.0, 1.0)
                )
                up = jnp.where(degree > orders, up, 0.0)
                onset = jnp.where(degree == orders, 1.0, 0.0)
                current = wide(up) * (cosine * first - wide(back) * second) + wide(onset)
                kept = jnp.where(jnp.full((16, PTS), degree, jnp.int32) <= LMAX, current * scale, 0.0)
                for part in range(PTS // 128):
                    table[part, pl.ds(pl.multiple_of(degree * 16, 16), 16), :] = kept[
                        :, part * 128 : part * 128 + 128
                    ]
                second = first
                first = current
            magnitude = jnp.maximum(jnp.abs(first), jnp.abs(second))
            factor = jnp.where(magnitude > 1.0, magnitude, 1.0)
            return first / factor, second / factor, log_scale + jnp.log(factor)

        zero = jnp.zeros((16, PTS), F32)
        lax.fori_loop(0, 23, block, (zero, zero, start))
        table[:, pl.ds(368 * 16, 16 * 16), :] = jnp.zeros((PTS // 128, 256, 128), F32)

    for part in range(PTS // 128):
        lanes = slice(part * 128, part * 128 + 128)
        values = table[part, pl.ds(step, DEG, stride=16), :]
        leg_ref[0, :, lanes] = values.astype(BF16)
        legt_ref[0, lanes, :] = values.T.astype(BF16)


def legendre(first_order, geo, diag):
    return pl.pallas_call(
        legendre_kernel,
        grid=(MDEV,),
        in_specs=[SMEM, whole((8, PTS)), whole((16, 128))],
        out_specs=[
            pl.BlockSpec((1, DEG, PTS), lambda m: (m, 0, 0)),
            pl.BlockSpec((1, PTS, DEG), lambda m: (m, 0, 0)),
        ],
        out_shape=[
            jax.ShapeDtypeStruct((MDEV, DEG, PTS), BF16),
            jax.ShapeDtypeStruct((MDEV, PTS, DEG), BF16),
        ],
        scratch_shapes=[pltpu.VMEM((PTS // 128, DEG * 16, 128), F32)],
        compiler_params=params(),
        name="legendre",
    )(first_order, geo, diag)


def window(row):
    start = row * FIELDS
    return start // 128 * 128, start % 128


def order_factor(first_ref):
    order = first_ref[0] + pl.program_id(0)
    edge = jnp.logical_or(order == 0, order == LMAX)
    return jnp.where(edge, 1.0, 2.0)


def forward_kernel(
    first_ref, z_ref, leg_ref, legt_ref, enc_ref, mix_ref, gain_ref, out_ref, rows, points, made
):
    step = pl.program_id(0)

    @pl.when(step == 0)
    def _():
        for r in range(BAND):
            base, off = window(r)
            pair = z_ref[:, base : base + 256].astype(F32)
            rows[r] = pltpu.roll(pair, (256 - off) % 256, 1)[:, :128]
        points[...] = jnp.zeros((PTS, 256), BF16)

    for r in range(BAND):
        for k in range(2):
            got = rows[r, pl.ds(k * MDEV + step, BANDS, stride=KM), :]
            points[r * BANDS : (r + 1) * BANDS, k * 128 : (k + 1) * 128] = got.astype(BF16)
    coeffs = dot(leg_ref[0], points[...], 1, 0).astype(BF16)
    factor = order_factor(first_ref)
    gain = gain_ref[...] * factor
    filtered = []
    for k in range(2):
        channels = dot(coeffs[:, k * 128 : (k + 1) * 128], enc_ref[...], 1, 0).astype(BF16)
        filtered.append((dot(channels, mix_ref[...], 1, 0) * gain).astype(BF16))
    synth = dot(legt_ref[0], jnp.concatenate(filtered, axis=1), 1, 0)
    for r in range(BAND):
        for k in range(2):
            made[r, pl.ds(k * MDEV + step, BANDS, stride=KM), :] = synth[
                r * BANDS : (r + 1) * BANDS, k * 128 : (k + 1) * 128
            ]

    @pl.when(step == MDEV - 1)
    def _():
        for r in range(BAND):
            out_ref[:, r * CH : (r + 1) * CH] = made[r].astype(BF16)


def backward_kernel(
    first_ref, z_ref, leg_ref, legt_ref, enct_ref, mixt_ref, gain_ref, out_ref, rows, points, made
):
    step = pl.program_id(0)

    @pl.when(step == 0)
    def _():
        for r in range(BAND):
            rows[r] = z_ref[:, r * CH : (r + 1) * CH].astype(F32)
        points[...] = jnp.zeros((PTS, 256), BF16)

    for r in range(BAND):
        for k in range(2):
            got = rows[r, pl.ds(k * MDEV + step, BANDS, stride=KM), :]
            points[r * BANDS : (r + 1) * BANDS, k * 128 : (k + 1) * 128] = got.astype(BF16)
    grads = dot(leg_ref[0], points[...], 1, 0)
    gain = gain_ref[...] * order_factor(first_ref)
    back = []
    for k in range(2):
        scaled = (grads[:, k * 128 : (k + 1) * 128] * gain).astype(BF16)
        channels = dot(scaled, mixt_ref[...], 1, 0).astype(BF16)
        back.append(dot(channels, enct_ref[...], 1, 0).astype(BF16))
    synth = dot(legt_ref[0], jnp.concatenate(back, axis=1), 1, 0)
    for r in range(BAND):
        for k in range(2):
            made[r, pl.ds(k * MDEV + step, BANDS, stride=KM), :] = synth[
                r * BANDS : (r + 1) * BANDS, k * 128 : (k + 1) * 128
            ]

    @pl.when(step == MDEV - 1)
    def _():
        low = jnp.zeros((BANDS * KM, 128), F32)
        at = 0
        for r in range(BAND):
            base, off = window(r)
            while at < base:
                out_ref[:, at : at + 128] = low.astype(BF16)
                low = spill
                at += 128
            value = made[r]
            pair = jnp.concatenate([value, jnp.zeros_like(value)], axis=1)
            moved = pltpu.roll(pair, off, 1)
            low = low + moved[:, :128]
            spill = moved[:, 128:]
        out_ref[:, at : at + 128] = low.astype(BF16)
        at += 128
        out_ref[:, at : at + 128] = spill.astype(BF16)


def spectral(kernel, lanes_out, first_order, z, leg, legt, first_w, second_w, gain):
    return pl.pallas_call(
        kernel,
        grid=(MDEV,),
        in_specs=[
            SMEM,
            whole(z.shape),
            pl.BlockSpec((1, DEG, PTS), lambda m: (m, 0, 0)),
            pl.BlockSpec((1, PTS, DEG), lambda m: (m, 0, 0)),
            whole((128, 128)),
            whole((128, 128)),
            whole((DEG, CH)),
        ],
        out_specs=whole((BANDS * KM, lanes_out)),
        out_shape=jax.ShapeDtypeStruct((BANDS * KM, lanes_out), BF16),
        scratch_shapes=[
            pltpu.VMEM((BAND, BANDS * KM, 128), F32),
            pltpu.VMEM((PTS, 256), BF16),
            pltpu.VMEM((BAND, BANDS * KM, 128), F32),
        ],
        compiler_params=params(),
        name=kernel.__name__,
    )(first_order, z, leg, legt, first_w, second_w, gain)


def grid_kernel(live_ref, s_ref, c_ref, x_ref, enct_ref, dect_ref, pred_ref, slope_ref):
    step = pl.program_id(0)
    for part in range(3):
        lanes = slice(part * CH, (part + 1) * CH)
        field = dot(s_ref[:, lanes], c_ref[...], 0, 0)
        live = live_ref[step * 3 + part]
        state = x_ref[part]
        hidden = (dot(enct_ref[...], state, 1, 0) * live).astype(BF16).astype(F32)
        cdf = 0.5 * (1.0 + lax.erf(field * (1.0 / math.sqrt(2.0))))
        slope = cdf + field * jnp.exp(-0.5 * field * field) * (1.0 / math.sqrt(2.0 * math.pi))
        block = ((field * cdf + hidden) * live).astype(BF16)
        decoded = dot(dect_ref[...], block, 1, 0)
        pred_ref[part] = ((state.astype(F32) + decoded) * live).astype(BF16)
        slope_ref[part] = slope.astype(BF16)


def grid_stage(live, s, c, x, enct, dect):
    return pl.pallas_call(
        grid_kernel,
        grid=(5,),
        in_specs=[
            SMEM,
            pl.BlockSpec((BANDS * KM, 3 * CH), lambda g: (0, g)),
            whole((BANDS * KM, NLON)),
            pl.BlockSpec((3, FIELDS, NLON), lambda g: (g, 0, 0)),
            whole((CH, FIELDS)),
            whole((FIELDS, CH)),
        ],
        out_specs=[
            pl.BlockSpec((3, FIELDS, NLON), lambda g: (g, 0, 0)),
            pl.BlockSpec((3, CH, NLON), lambda g: (g, 0, 0)),
        ],
        out_shape=[
            jax.ShapeDtypeStruct((16, FIELDS, NLON), BF16),
            jax.ShapeDtypeStruct((BAND, CH, NLON), BF16),
        ],
        compiler_params=params(),
        name="grid_stage",
    )(live, s, c, x, enct, dect)


def score_kernel(area_ref, p_ref, o_ref, out_ref):
    area = area_ref[pl.program_id(0)]
    values = [p_ref[e, 0].astype(F32) for e in range(MEMBERS)]
    truth = o_ref[0].astype(F32)

    def inverse(gap):
        return lax.rsqrt(jnp.sum(gap * gap, axis=0, keepdims=True) + EPSILON)

    weights = {}
    for e in range(MEMBERS):
        for f in range(e):
            weights[e, f] = weights[f, e] = inverse(values[e] - values[f]) * (area / MEMBERS)
    for e in range(MEMBERS):
        gap = values[e] - truth
        total = gap * (inverse(gap) * area)
        for f in range(MEMBERS):
            if f != e:
                total = total - (values[e] - values[f]) * weights[e, f]
        out_ref[e, 0] = total.astype(BF16)


def score_stage(area, everyone, truth):
    return pl.pallas_call(
        score_kernel,
        grid=(2, 6),
        in_specs=[
            SMEM,
            pl.BlockSpec((MEMBERS, 1, FIELDS, 128), lambda r, j: (0, r, 0, j)),
            pl.BlockSpec((1, FIELDS, 128), lambda r, j: (r, 0, j)),
        ],
        out_specs=pl.BlockSpec((MEMBERS, 1, FIELDS, 128), lambda r, j: (0, r, 0, j)),
        out_shape=jax.ShapeDtypeStruct((MEMBERS, 2, FIELDS, NLON), BF16),
        compiler_params=pltpu.CompilerParams(dimension_semantics=("arbitrary", "arbitrary")),
        name="score_stage",
    )(area, everyone, truth)


def grad_kernel(g_ref, slope_ref, c_ref, dec_ref, out_ref):
    fields = []
    for part in range(3):
        block = dot(dec_ref[...], g_ref[part], 1, 0)
        fields.append((block * slope_ref[part].astype(F32)).astype(BF16))
    out_ref[...] = dot(c_ref[...], jnp.concatenate(fields, axis=0), 1, 1).astype(BF16)


def grad_stage(score, slope, c, dec):
    return pl.pallas_call(
        grad_kernel,
        grid=(5,),
        in_specs=[
            pl.BlockSpec((3, FIELDS, NLON), lambda g: (g, 0, 0)),
            pl.BlockSpec((3, CH, NLON), lambda g: (g, 0, 0)),
            whole((BANDS * KM, NLON)),
            whole((CH, FIELDS)),
        ],
        out_specs=pl.BlockSpec((BANDS * KM, 3 * CH), lambda g: (0, g)),
        out_shape=jax.ShapeDtypeStruct((BANDS * KM, WIDE), BF16),
        compiler_params=params(),
        name="grad_stage",
    )(score, slope, c, dec)


def final_kernel(weight_ref, live_ref, z_ref, c_ref, g_ref, dec_ref, enc_ref, out_ref, spread):
    spread[...] = dot(z_ref[...], c_ref[...], 0, 0)
    for r in range(BAND):
        score = g_ref[r]
        block = dot(dec_ref[...], score, 1, 0).astype(BF16)
        local = dot(enc_ref[...], block, 1, 0)
        far = spread[r * FIELDS : (r + 1) * FIELDS, :] * weight_ref[r]
        out_ref[r] = ((score.astype(F32) + local + far) * live_ref[r]).astype(BF16)


def final_stage(weight, live, z, c, score, dec, enc):
    return pl.pallas_call(
        final_kernel,
        in_specs=[SMEM, SMEM] + [pl.BlockSpec(memory_space=pltpu.VMEM)] * 5,
        out_specs=pl.BlockSpec(memory_space=pltpu.VMEM),
        out_shape=jax.ShapeDtypeStruct((BAND, FIELDS, NLON), BF16),
        scratch_shapes=[pltpu.VMEM((FLAT, NLON), F32)],
        compiler_params=pltpu.CompilerParams(vmem_limit_bytes=56 * 1024 * 1024),
        name="final_stage",
    )(weight, live, z, c, score, dec, enc)


def exchange(array, axis):
    return lax.all_to_all(array, axis, split_axis=0, concat_axis=0, tiled=True)


def on_device(
    states, observed, band_rows, encoder_weight, mixing_weight, degree_gain, decoder_weight
):
    band = lax.axis_index("space")
    member = lax.axis_index("member")
    first = band * MDEV

    number = jnp.arange(BANDS, dtype=jnp.int32)
    point = jnp.arange(PTS, dtype=jnp.int32)
    point_band, point_row = point % BANDS, point // BANDS
    starts = jnp.sum(jnp.where(number[:, None] < point_band[None], band_rows[:, None], 0), axis=0)
    counts = jnp.sum(jnp.where(number[:, None] == point_band[None], band_rows[:, None], 0), axis=0)
    colatitude = jnp.minimum(starts + point_row, NLAT - 1).astype(F32) * (math.pi / (NLAT - 1))
    log_sine = jnp.log(jnp.maximum(jnp.sin(colatitude), 1e-30))
    live = (point_row < counts).astype(F32)
    zero = jnp.zeros_like(live)
    geo = jnp.stack([jnp.cos(colatitude), log_sine, live] + [zero] * 5)
    own_start = jnp.sum(jnp.where(number < band, band_rows, 0))
    own_count = jnp.sum(jnp.where(number == band, band_rows, 0))
    row = jnp.arange(16, dtype=jnp.int32)
    own_live = (row < own_count).astype(F32)
    own_lat = jnp.minimum(own_start + row, NLAT - 1).astype(F32) * (math.pi / (NLAT - 1))
    own_sine = jnp.sin(own_lat)
    own_weight = own_live * own_sine * (math.pi / (NLAT - 1) / NLON)
    own_area = 8.0 * own_sine * own_live
    first_order = first.reshape(1)

    c = fourier_table()
    diag = lax.dynamic_slice_in_dim(jnp.asarray(diagonal_logs()), first, 16)
    diag = jnp.broadcast_to(diag[:, None], (16, 128))
    gain = jnp.pad(degree_gain, ((0, DEG - degree_gain.shape[0]), (0, 0)))
    enc = encoder_weight
    enct = enc.T
    dec = decoder_weight
    dect = dec.T
    enc_wide = jnp.pad(enc, ((0, 128 - FIELDS), (0, 0)))
    enct_wide = enc_wide.T

    x = jnp.transpose(states[0], (1, 0, 2))
    flat = jnp.pad(x.reshape(BAND * FIELDS, NLON), ((0, FLAT - BAND * FIELDS), (0, 0)))
    lane_row = jnp.arange(FLAT, dtype=jnp.int32) // FIELDS
    lane_weight = jnp.sum(jnp.where(row[:, None] == lane_row[None], own_weight[:, None], 0.0), axis=0)
    zonal = (
        jnp.einsum("aj,bj->ab", c, flat, preferred_element_type=F32) * lane_weight[None]
    ).astype(BF16)

    arrived = exchange(zonal, "space")
    leg, legt = legendre(first_order, geo, diag)
    synth = spectral(
        forward_kernel, WIDE, first_order, arrived, leg, legt, enc_wide, mixing_weight, gain
    )
    synth = exchange(synth, "space")
    predicted, slope = grid_stage(own_live, synth, c, x, enct, dect)

    everyone = exchange(predicted, "member").reshape(MEMBERS, 2, FIELDS, NLON)
    padded = jnp.pad(observed, ((0, 0), (0, 1), (0, 0)))
    truth = jnp.transpose(lax.dynamic_slice_in_dim(padded, member * 2, 2, 1), (1, 0, 2))
    area = lax.dynamic_slice_in_dim(own_area, member * 2, 2)
    share = score_stage(area, everyone, truth)
    score = exchange(share.reshape(16, FIELDS, NLON), "member")

    grads = exchange(grad_stage(score, slope, c, dec), "space")
    grads = spectral(
        backward_kernel, FLAT, first_order, grads, leg, legt, enct_wide, mixing_weight.T, gain
    )
    grads = exchange(grads, "space")
    result = final_stage(own_weight, own_live, grads, c, score, dec, enc)
    prediction = jnp.transpose(predicted[:BAND], (1, 0, 2))[None]
    return (prediction, jnp.transpose(result, (1, 0, 2))[None])


def solution(mesh):
    in_specs = (P("member", None, "space", None), P(None, "space", None), P(), P(), P(), P(), P())
    out_specs = (P("member", None, "space", None), P("member", None, "space", None))
    return jax.shard_map(
        on_device, mesh=mesh, in_specs=in_specs, out_specs=out_specs, check_vma=False
    )
```

time: 704 us -> 408 us (0.58)
  other arithmetic: 161 us -> 4.73 us
  blocking collectives: 109 us -> 0 us
  local copies, waits for them, and re-layouts: 129 us -> 27.7 us
  Pallas kernels: 0 us -> 90.2 us
  matrix products: 73.6 us -> 4.39 us
  waiting for transfers between devices: 175 us -> 239 us
    all_to_all x2 -> x0, blocking collectives: 109 us -> none  [the longest x1 75.6 us: to_bands(): lax.all_to_all(block, 'space', split_axis=2, concat_axis=1, tiled=True)]
    pallas_call x0 -> x7, Pallas kernels: none -> 90.2 us  [the longest x2 37.5 us: spectral(): pl.pallas_call(kernel, grid=(MDEV,), in_specs=[SMEM, whole(z.shape), pl.B...]
    dot_general x13 -> x1, matrix products: 73.6 us -> 4.39 us  [on_device(): jnp.einsum('aj,bj->ab', c, flat, preferred_element_type=F32)]
    all_to_all x6, waiting for transfers between devices: 175 us -> 239 us  [exchange(): return lax.all_to_all(array, axis, split_axis=0, concat_axis=0, tiled=True)]
    add x34 -> x0, other arithmetic: 54.7 us -> none  [the longest x8 52.2 us: accumulate(): return (running + member_gap / member_dist, None)]
    while x345 -> x0, other arithmetic: 31.4 us -> none
    slice x7 -> x0, local copies, waits for them, and re-layouts: 27.3 us -> none  [the longest x6 27.2 us: grouped_exchange(): lax.slice_in_dim(a, low, high, axis=item_dim)]
    reduce_sum x10 -> x3, other arithmetic: 26 us -> 0.88 us  [the longest x1 0.69 us: on_device(): own_start = jnp.sum(jnp.where(number < band, band_rows, 0))]
  transfers between devices with their start and end apart: 6 -> 6, of which waited for: 5 -> 6; matrix products, arithmetic and copies ran while one was open for 18% -> 4% of each run, Pallas kernels for 0% -> 4%
where the time goes in v1:
time: 408 us; the launch traced here: 404 us
  waiting for transfers between devices  239 us (59%)
  Pallas kernels  90.2 us (22%)
  starting transfers between devices  37.6 us (9%)
  local copies, waits for them, and re-layouts  27.7 us (7%)
  other arithmetic  4.73 us (1%)
  matrix products  4.39 us (1%)
    all_to_all x6, waiting for transfers between devices, exchange(): return lax.all_to_all(array, axis, split_axis=0, concat_axis=0, tiled=True)  239 us
    all_to_all x6, starting transfers between devices, exchange(): return lax.all_to_all(array, axis, split_axis=0, concat_axis=0, tiled=True)  37.6 us
    pallas_call x2, Pallas kernels, spectral(): pl.pallas_call(kernel, grid=(MDEV,), in_specs=[SMEM, whole(z.shape), pl.B...  37.5 us
    unnamed x40, local copies, waits for them, and re-layouts  19.2 us
    pallas_call x1, Pallas kernels, legendre(): pl.pallas_call(legendre_kernel, grid=(MDEV,), in_specs=[SMEM, whole((8, P...  16 us
    pallas_call x1, Pallas kernels, grid_stage(): pl.pallas_call(grid_kernel, grid=(5,), in_specs=[SMEM, pl.BlockSpec((BAND...  10.2 us
    pallas_call x1, Pallas kernels, score_stage(): pl.pallas_call(score_kernel, grid=(2, 6), in_specs=[SMEM, pl.BlockSpec((M...  10.1 us
    pallas_call x1, Pallas kernels, grad_stage(): pl.pallas_call(grad_kernel, grid=(5,), in_specs=[pl.BlockSpec((3, FIELDS,...  8.34 us
  transfers between devices with their start and end apart: 6, of which 6 were waited for; matrix products, arithmetic and copies ran while one was open for 4% of the time, Pallas kernels for 4%

profile of v1, /device:TPU:7, one launch (start us, length us, event | category | flops | bytes accessed | tf_op | source)
XLA Modules:
  0.0 404.2 jit_solution(4814196162227893768)
XLA Ops:
  0.6 2.0 copy.43
  2.7 0.0 copy-start.1
  2.7 0.0 copy-start.15
  2.7 0.0 copy-start.4
  2.7 2.0 reshape.140
  4.7 0.0 copy-done.15
  4.7 0.7 fusion.10
  5.4 1.3 select_multiply_fusion.weight_ref
  6.7 0.0 copy-start.14
  6.7 0.1 select_reduce_fusion
  6.8 0.0 copy-done.4
  6.8 4.4 %fusion = bf16[1152,768]{0,1:T(8,128)(2,1)} fusion(bf16[768,720]{1,0:T(8,128)(2,1)S(1)} %copy-done.4, f32[1152]{0:T(1024)S(1)} %select_reduce_fusion, bf16[1095,720]{1,0:T(8,128)(2,1)} %reshape.140), kind=kOutput, calls=%fused_computation.1 | convolution fusion | flops 1275789312 | bytes 4456800 | tf_op jit(solution)/shard_map/aj,bj->ab/dot_general | solution.py:433
  11.2 0.0 copy-done.1
  11.2 0.0 copy-done.14
  11.2 11.1 %all-to-all-start = ((bf16[32,24,1152]{2,1,0:T(8,128)(2,1)}), bf16[32,24,1152]{2,1,0:T(8,128)(2,1)S(1)}, u32[]{:S(2)}, u32[]{:S(2)}) async-start(bf16[32,24,1152]{2,1,0:T(8,128)(2,1)} %bitcast.46), calls=%async_computation | async-start | bytes 3538944 | tf_op jit(solution)/shard_map/all_to_all | solution.py:387
  22.4 0.0 copy-done.12
  22.4 0.1 copy.32
  22.5 0.1 copy.42
  22.6 0.8 dynamic_slice.9
  23.4 0.6 pad.17.clone.enc_ref
  24.0 0.0 copy-done.10
  24.0 0.7 pad.18.gain_ref
  24.7 0.1 select_reduce_fusion.1
  24.8 0.1 maximum_log_fusion
  25.0 0.6 stack.10.geo_ref
  25.6 0.7 broadcast_in_dim.60.diag_ref
  26.2 16.0 %legendre.1 = (bf16[12,384,512]{2,1,0:T(8,128)(2,1)}, bf16[12,512,384]{2,1,0:T(8,128)(2,1)}) custom-call(s32[1]{0:T(128)} %bitcast.first_ref, f32[8,512]{1,0:T(8,128)} %stack.10.geo_ref, f32[16,128]{1,0:T(8,128)} %broadcast_in_dim.60.diag_ref), custom_call_target="tpu_custom_call" | custom-call | tf_op jit(solution)/shard_map/legendre/pallas_call | solution.py:121
  42.2 23.4 %all-to-all-done = bf16[32,24,1152]{2,1,0:T(8,128)(2,1)S(1)} async-done(((bf16[32,24,1152]{2,1,0:T(8,128)(2,1)}), bf16[32,24,1152]{2,1,0:T(8,128)(2,1)S(1)}, u32[]{:S(2)}, u32[]{:S(2)}) %all-to-all-start) | async-done | bytes 1769504 | tf_op jit(solution)/shard_map/all_to_all | solution.py:387
  65.7 1.2 copy-done.7
  66.9 18.4 %forward_kernel.1 = bf16[768,1920]{1,0:T(8,128)(2,1)} custom-call(s32[1]{0:T(128)} %bitcast.first_ref, bf16[768,1152]{1,0:T(8,128)(2,1)} %bitcast.44, bf16[12,384,512]{2,1,0:T(8,128)(2,1)} %get-tuple-element.6.leg_ref, bf16[12,512,384]{2,1,0:T(8,128)(2,1)} %get-tuple-element.7.legt_ref, bf16[128,128]{1,0:T(8,128)(2,1)} %pad.17.clone.enc_ref, ...), custom_call_target="tpu_custom_call" | custom-call | tf_op jit(solution)/shard_map/forward_kernel/pallas_call | solution.py:237
  85.3 0.0 copy-done.8
  85.3 4.6 %all-to-all-start.1 = ((bf16[32,24,1920]{2,1,0:T(8,128)(2,1)}), bf16[32,24,1920]{2,1,0:T(8,128)(2,1)S(1)}, u32[]{:S(2)}, u32[]{:S(2)}) async-start(bf16[32,24,1920]{2,1,0:T(8,128)(2,1)} %bitcast.40), calls=%async_computation.1 | async-start | bytes 5898240 | tf_op jit(solution)/shard_map/all_to_all | solution.py:387
  89.9 1.1 fusion.11.live_ref
  91.1 66.7 %all-to-all-done.1 = bf16[32,24,1920]{2,1,0:T(8,128)(2,1)S(1)} async-done(((bf16[32,24,1920]{2,1,0:T(8,128)(2,1)}), bf16[32,24,1920]{2,1,0:T(8,128)(2,1)S(1)}, u32[]{:S(2)}, u32[]{:S(2)}) %all-to-all-start.1) | async-done | bytes 2949152 | tf_op jit(solution)/shard_map/all_to_all | solution.py:387
  157.8 1.6 copy-done.3
  159.4 10.2 %grid_stage.1 = (bf16[16,73,720]{2,1,0:T(8,128)(2,1)}, bf16[15,128,720]{2,1,0:T(8,128)(2,1)}) custom-call(f32[16]{0:T(128)} %fusion.11.live_ref, bf16[768,1920]{1,0:T(8,128)(2,1)} %bitcast.38, bf16[768,720]{1,0:T(8,128)(2,1)} %constant.86.clone.c_ref, bf16[15,73,720]{2,1,0:T(8,128)(2,1)} %bitcast.36, bf16[128,73]{1,0:T(8,128)(2,1)} %bitcast.47, ...), custom_call_target="tpu_custom_call" | custom-call | tf_op jit(solution)/shard_map/grid_stage/pallas_call | solution.py:278
  169.6 6.6 %all-to-all-start.2 = ((bf16[16,73,720]{2,1,0:T(8,128)(2,1)}), bf16[16,73,720]{2,1,0:T(8,128)(2,1)S(1)}, u32[]{:S(2)}, u32[]{:S(2)}) async-start(bf16[16,73,720]{2,1,0:T(8,128)(2,1)} %get-tuple-element.8), calls=%async_computation.2 | async-start | bytes 3932160 | tf_op jit(solution)/shard_map/all_to_all | solution.py:387
  176.2 3.4 copy.35
  179.6 1.3 multiply_select_fusion
  180.9 0.7 dynamic_slice.10.area_ref
  181.5 1.7 fusion.2.o_ref
  183.2 17.8 %all-to-all-done.2 = bf16[16,73,720]{2,1,0:T(8,128)(2,1)S(1)} async-done(((bf16[16,73,720]{2,1,0:T(8,128)(2,1)}), bf16[16,73,720]{2,1,0:T(8,128)(2,1)S(1)}, u32[]{:S(2)}, u32[]{:S(2)}) %all-to-all-start.2) | async-done | bytes 1681952 | tf_op jit(solution)/shard_map/all_to_all | solution.py:387
  201.0 1.3 copy-done.5
  202.3 10.1 %score_stage.1 = bf16[8,2,73,720]{3,2,1,0:T(8,128)(2,1)} custom-call(f32[2]{0:T(128)} %dynamic_slice.10.area_ref, bf16[8,2,73,720]{3,2,1,0:T(8,128)(2,1)} %bitcast.41, bf16[2,73,720]{2,1,0:T(8,128)(2,1)} %fusion.2.o_ref), custom_call_target="tpu_custom_call" | custom-call | tf_op jit(solution)/shard_map/score_stage/pallas_call | solution.py:324
  212.4 4.6 %all-to-all-start.3 = ((bf16[16,73,720]{2,1,0:T(8,128)(2,1)}), bf16[16,73,720]{2,1,0:T(8,128)(2,1)S(1)}, u32[]{:S(2)}, u32[]{:S(2)}) async-start(bf16[16,73,720]{2,1,0:T(8,128)(2,1)} %bitcast.42), calls=%async_computation.3 | async-start | bytes 3932160 | tf_op jit(solution)/shard_map/all_to_all | solution.py:387
  217.0 0.0 copy-done.13
  217.0 0.7 copy.36.dec_ref
  217.7 24.1 %all-to-all-done.3.g_ref = bf16[16,73,720]{2,1,0:T(8,128)(2,1)S(1)} async-done(((bf16[16,73,720]{2,1,0:T(8,128)(2,1)}), bf16[16,73,720]{2,1,0:T(8,128)(2,1)S(1)}, u32[]{:S(2)}, u32[]{:S(2)}) %all-to-all-start.3) | async-done | bytes 1681952 | tf_op jit(solution)/shard_map/all_to_all | solution.py:387
  241.8 1.4 copy-done
  243.2 8.3 %grad_stage.1 = bf16[768,1920]{1,0:T(8,128)(2,1)} custom-call(bf16[16,73,720]{2,1,0:T(8,128)(2,1)} %copy-done, bf16[15,128,720]{2,1,0:T(8,128)(2,1)} %get-tuple-element.9.slope_ref, bf16[768,720]{1,0:T(8,128)(2,1)} %constant.86.clone.c_ref, bf16[128,73]{1,0:T(8,128)(2,1)} %copy.36.dec_ref), custom_call_target="tpu_custom_call" | custom-call | tf_op jit(solution)/shard_map/grad_stage/pallas_call | solution.py:348
  251.5 5.1 %all-to-all-start.4 = ((bf16[32,24,1920]{2,1,0:T(8,128)(2,1)}), bf16[32,24,1920]{2,1,0:T(8,128)(2,1)S(1)}, u32[]{:S(2)}, u32[]{:S(2)}) async-start(bf16[32,24,1920]{2,1,0:T(8,128)(2,1)} %bitcast.39), calls=%async_computation.4 | async-start | bytes 5898240 | tf_op jit(solution)/shard_map/all_to_all | solution.py:387
  256.7 0.7 copy.37
  257.4 0.0 copy-done.9
  257.4 0.6 pad_bitcast_fusion.enct_ref
  258.0 66.8 %all-to-all-done.4 = bf16[32,24,1920]{2,1,0:T(8,128)(2,1)S(1)} async-done(((bf16[32,24,1920]{2,1,0:T(8,128)(2,1)}), bf16[32,24,1920]{2,1,0:T(8,128)(2,1)S(1)}, u32[]{:S(2)}, u32[]{:S(2)}) %all-to-all-start.4) | async-done | bytes 2949152 | tf_op jit(solution)/shard_map/all_to_all | solution.py:387
  324.8 1.6 copy-done.2
  326.4 19.1 %backward_kernel.1 = bf16[768,1152]{1,0:T(8,128)(2,1)} custom-call(s32[1]{0:T(128)} %bitcast.first_ref, bf16[768,1920]{1,0:T(8,128)(2,1)} %bitcast.37, bf16[12,384,512]{2,1,0:T(8,128)(2,1)} %get-tuple-element.6.leg_ref, bf16[12,512,384]{2,1,0:T(8,128)(2,1)} %get-tuple-element.7.legt_ref, bf16[128,128]{1,0:T(8,128)(2,1)} %pad_bitcast_fusion.enct_ref, ...), custom_call_target="tpu_custom_call" | custom-call | tf_op jit(solution)/shard_map/backward_kernel/pallas_call | solution.py:237
  345.5 5.5 %all-to-all-start.5 = ((bf16[32,24,1152]{2,1,0:T(8,128)(2,1)}), bf16[32,24,1152]{2,1,0:T(8,128)(2,1)}, u32[]{:S(2)}, u32[]{:S(2)}) async-start(bf16[32,24,1152]{2,1,0:T(8,128)(2,1)} %bitcast.45), calls=%async_computation.5 | async-start | bytes 3538944 | tf_op jit(solution)/shard_map/all_to_all | solution.py:387
  350.9 0.0 copy-done.6
  351.0 0.1 slice_bitcast_fusion
  351.1 1.8 copy.39
  352.8 40.0 %all-to-all-done.5 = bf16[32,24,1152]{2,1,0:T(8,128)(2,1)} async-done(((bf16[32,24,1152]{2,1,0:T(8,128)(2,1)}), bf16[32,24,1152]{2,1,0:T(8,128)(2,1)}, u32[]{:S(2)}, u32[]{:S(2)}) %all-to-all-start.5) | async-done | bytes 1769504 | tf_op jit(solution)/shard_map/all_to_all | solution.py:387
  392.8 8.1 %final_stage.1 = bf16[15,73,720]{2,1,0:T(8,128)(2,1)} custom-call(f32[16]{0:T(128)} %copy-done.14, f32[16]{0:T(128)} %fusion.11.live_ref, bf16[768,1152]{1,0:T(8,128)(2,1)} %bitcast.22.z_ref, bf16[768,720]{1,0:T(8,128)(2,1)} %constant.86.clone.c_ref, bf16[16,73,720]{2,1,0:T(8,128)(2,1)} %copy-done, bf16[128,73]{1,0:T(8,128)(2,1)} %copy.36.dec_ref, ...), custom_call_target="tpu_custom_call" | custom-call | tf_op jit(solution)/shard_map/final_stage/pallas_call | solution.py:375
  401.0 3.3 copy.40
  (18 shorter events, 0.1 us)
Async XLA Ops:
  2.7 8.5 %copy-start.1 = (bf16[1,73,15,720]{3,1,2,0:T(8,128)(2,1)}, bf16[1,73,15,720]{3,1,2,0:T(8,128)(2,1)S(1)}, u32[]{:S(2)}) copy-start(bf16[1,73,15,720]{3,1,2,0:T(8,128)(2,1)S(1)} %copy.43) | copy-start | bytes 4730404
  2.7 2.0 copy-start.15
  2.7 4.1 %copy-start.4 = (bf16[768,720]{1,0:T(8,128)(2,1)S(1)}, bf16[768,720]{1,0:T(8,128)(2,1)}, u32[]{:S(2)}) copy-start(bf16[768,720]{1,0:T(8,128)(2,1)} %constant.86.clone.c_ref) | copy-start | bytes 3317764
  6.7 4.5 %copy-start.14 = (f32[16]{0:T(128)}, f32[16]{0:T(128)S(1)}, u32[]{:S(2)}) copy-start(f32[16]{0:T(128)S(1)} %select_multiply_fusion.weight_ref) | copy-start | bytes 196
  11.2 11.2 %copy-start.12 = (bf16[73,128]{1,0:T(8,128)(2,1)S(1)}, bf16[73,128]{1,0:T(8,128)(2,1)}, u32[]{:S(2)}) copy-start(bf16[73,128]{1,0:T(8,128)(2,1)} %enc_ref.1) | copy-start | bytes 56068
  11.2 12.8 %copy-start.10 = (f32[368,128]{1,0:T(8,128)S(1)}, f32[368,128]{1,0:T(8,128)}, u32[]{:S(2)}) copy-start(f32[368,128]{1,0:T(8,128)} %param.14) | copy-start | bytes 565252
  11.2 54.4 %all-to-all-start = ((bf16[32,24,1152]{2,1,0:T(8,128)(2,1)}), bf16[32,24,1152]{2,1,0:T(8,128)(2,1)S(1)}, u32[]{:S(2)}, u32[]{:S(2)}) async-start(bf16[32,24,1152]{2,1,0:T(8,128)(2,1)} %bitcast.46), calls=%async_computation | async-start | bytes 3538944 | tf_op jit(solution)/shard_map/all_to_all | solution.py:387
  22.5 62.8 %copy-start.8 = (bf16[73,128]{0,1:T(8,128)(2,1)}, bf16[73,128]{0,1:T(8,128)(2,1)S(1)}, u32[]{:S(2)}) copy-start(bf16[73,128]{0,1:T(8,128)(2,1)S(1)} %copy.32) | copy-start | bytes 56068
  65.7 1.2 copy-start.7
  85.3 72.5 %all-to-all-start.1 = ((bf16[32,24,1920]{2,1,0:T(8,128)(2,1)}), bf16[32,24,1920]{2,1,0:T(8,128)(2,1)S(1)}, u32[]{:S(2)}, u32[]{:S(2)}) async-start(bf16[32,24,1920]{2,1,0:T(8,128)(2,1)} %bitcast.40), calls=%async_computation.1 | async-start | bytes 5898240 | tf_op jit(solution)/shard_map/all_to_all | solution.py:387
  157.8 1.6 copy-start.3
  169.6 31.4 %all-to-all-start.2 = ((bf16[16,73,720]{2,1,0:T(8,128)(2,1)}), bf16[16,73,720]{2,1,0:T(8,128)(2,1)S(1)}, u32[]{:S(2)}, u32[]{:S(2)}) async-start(bf16[16,73,720]{2,1,0:T(8,128)(2,1)} %get-tuple-element.8), calls=%async_computation.2 | async-start | bytes 3932160 | tf_op jit(solution)/shard_map/all_to_all | solution.py:387
  201.0 1.3 copy-start.5
  212.4 4.6 %copy-start.13 = (bf16[128,73]{0,1:T(8,128)(2,1)S(1)}, bf16[128,73]{0,1:T(8,128)(2,1)}, u32[]{:S(2)}) copy-start(bf16[128,73]{0,1:T(8,128)(2,1)} %param.15) | copy-start | bytes 56068
  212.4 29.4 %all-to-all-start.3 = ((bf16[16,73,720]{2,1,0:T(8,128)(2,1)}), bf16[16,73,720]{2,1,0:T(8,128)(2,1)S(1)}, u32[]{:S(2)}, u32[]{:S(2)}) async-start(bf16[16,73,720]{2,1,0:T(8,128)(2,1)} %bitcast.42), calls=%async_computation.3 | async-start | bytes 3932160 | tf_op jit(solution)/shard_map/all_to_all | solution.py:387
  241.8 1.4 copy-start
  251.5 5.2 %copy-start.11 = (bf16[128,128]{1,0:T(8,128)(2,1)S(1)}, bf16[128,128]{1,0:T(8,128)(2,1)}, u32[]{:S(2)}) copy-start(bf16[128,128]{1,0:T(8,128)(2,1)} %mix_ref.1) | copy-start | bytes 98308
  251.5 5.9 %copy-start.9 = (bf16[73,128]{0,1:T(8,128)(2,1)S(1)}, bf16[73,128]{0,1:T(8,128)(2,1)}, u32[]{:S(2)}) copy-start(bf16[73,128]{0,1:T(8,128)(2,1)} %copy-done.8) | copy-start | bytes 56068
  251.5 73.2 %all-to-all-start.4 = ((bf16[32,24,1920]{2,1,0:T(8,128)(2,1)}), bf16[32,24,1920]{2,1,0:T(8,128)(2,1)S(1)}, u32[]{:S(2)}, u32[]{:S(2)}) async-start(bf16[32,24,1920]{2,1,0:T(8,128)(2,1)} %bitcast.39), calls=%async_computation.4 | async-start | bytes 5898240 | tf_op jit(solution)/shard_map/all_to_all | solution.py:387
  324.8 1.6 copy-start.2
  345.5 5.5 %copy-start.6 = (bf16[16,73,720]{2,1,0:T(8,128)(2,1)S(1)}, bf16[16,73,720]{2,1,0:T(8,128)(2,1)}, u32[]{:S(2)}) copy-start(bf16[16,73,720]{2,1,0:T(8,128)(2,1)} %get-tuple-element.8) | copy-start | bytes 5045764
  345.5 47.4 %all-to-all-start.5 = ((bf16[32,24,1152]{2,1,0:T(8,128)(2,1)}), bf16[32,24,1152]{2,1,0:T(8,128)(2,1)}, u32[]{:S(2)}, u32[]{:S(2)}) async-start(bf16[32,24,1152]{2,1,0:T(8,128)(2,1)} %bitcast.45), calls=%async_computation.5 | async-start | bytes 3538944 | tf_op jit(solution)/shard_map/all_to_all | solution.py:387

commit v2 on v1

--- a/solution.py
+++ b/solution.py
@@ -21,6 +21,10 @@
 DEG = 384
 PTS = 512
 KM = 2 * MDEV
+GROUPS = 3
+GM = MDEV // GROUPS
+GK = 2 * GM
+MESH = pl.DeviceIdType.MESH
 FLAT = 1152
 WIDE = BAND * CH
 
@@ -51,7 +55,8 @@
     angle = 2.0 * np.pi * ((orders[:, None] * np.arange(NLON)[None, :]) % NLON) / NLON
     live = (orders <= LMAX)[:, None]
     both = np.stack([np.where(live, np.cos(angle), 0.0), np.where(live, -np.sin(angle), 0.0)])
-    both = both.reshape(2, BANDS, MDEV, NLON).transpose(1, 0, 2, 3).reshape(BANDS * KM, NLON)
+    both = both.reshape(2, BANDS, GROUPS, GM, NLON).transpose(2, 1, 0, 3, 4)
+    both = both.reshape(BANDS * KM, NLON)
     return jnp.asarray(both.astype(np.float32), BF16)
 
 
@@ -63,77 +68,59 @@
     )
 
 
-def legendre_kernel(first_ref, geo_ref, diag_ref, leg_ref, legt_ref, table):
-    step = pl.program_id(0)
-
-    @pl.when(step == 0)
-    def _():
-        first_order = first_ref[0]
-        cosine = jnp.broadcast_to(geo_ref[0:1, :], (16, PTS))
-        log_sine = geo_ref[1:2, :]
-        live = jnp.broadcast_to(geo_ref[2:3, :], (16, PTS))
-        orders = first_order + lax.broadcasted_iota(jnp.int32, (16, 128), 0)
-        order_f = orders.astype(F32)
-        order_sq = order_f * order_f
-
-        def wide(x):
-            return jnp.concatenate([x] * (PTS // 128), axis=1)
-
-        start = wide(diag_ref[...]) + wide(order_f) * log_sine
-
-        def block(number, carry):
-            first, second, log_scale = carry
-            scale = jnp.exp(log_scale) * live
-            for position in range(16):
-                degree = number * 16 + position
-                lf = jnp.full((16, 128), degree, jnp.int32).astype(F32)
-                up = jnp.sqrt((4.0 * lf * lf - 1.0) / jnp.maximum(lf * lf - order_sq, 1.0))
-                lb = lf - 1.0
-                back = jnp.sqrt(
-                    jnp.maximum(lb * lb - order_sq, 0.0) / jnp.maximum(4.0 * lb * lb - 1.0, 1.0)
-                )
-                up = jnp.where(degree > orders, up, 0.0)
-                onset = jnp.where(degree == orders, 1.0, 0.0)
-                current = wide(up) * (cosine * first - wide(back) * second) + wide(onset)
-                kept = jnp.where(jnp.full((16, PTS), degree, jnp.int32) <= LMAX, current * scale, 0.0)
-                for part in range(PTS // 128):
-                    table[part, pl.ds(pl.multiple_of(degree * 16, 16), 16), :] = kept[
-                        :, part * 128 : part * 128 + 128
-                    ]
-                second = first
-                first = current
-            magnitude = jnp.maximum(jnp.abs(first), jnp.abs(second))
-            factor = jnp.where(magnitude > 1.0, magnitude, 1.0)
-            return first / factor, second / factor, log_scale + jnp.log(factor)
-
-        zero = jnp.zeros((16, PTS), F32)
-        lax.fori_loop(0, 23, block, (zero, zero, start))
-        table[:, pl.ds(368 * 16, 16 * 16), :] = jnp.zeros((PTS // 128, 256, 128), F32)
-
-    for part in range(PTS // 128):
-        lanes = slice(part * 128, part * 128 + 128)
-        values = table[part, pl.ds(step, DEG, stride=16), :]
-        leg_ref[0, :, lanes] = values.astype(BF16)
-        legt_ref[0, lanes, :] = values.T.astype(BF16)
-
-
-def legendre(first_order, geo, diag):
-    return pl.pallas_call(
-        legendre_kernel,
-        grid=(MDEV,),
-        in_specs=[SMEM, whole((8, PTS)), whole((16, 128))],
-        out_specs=[
-            pl.BlockSpec((1, DEG, PTS), lambda m: (m, 0, 0)),
-            pl.BlockSpec((1, PTS, DEG), lambda m: (m, 0, 0)),
-        ],
-        out_shape=[
-            jax.ShapeDtypeStruct((MDEV, DEG, PTS), BF16),
-            jax.ShapeDtypeStruct((MDEV, PTS, DEG), BF16),
-        ],
-        scratch_shapes=[pltpu.VMEM((PTS // 128, DEG * 16, 128), F32)],
-        compiler_params=params(),
-        name="legendre",
-    )(first_order, geo, diag)
+def legendre_rows(first_order, geo_ref, diag_ref, table):
+    cosine = jnp.broadcast_to(geo_ref[0:1, :], (16, PTS))
+    log_sine = geo_ref[1:2, :]
+    live = jnp.broadcast_to(geo_ref[2:3, :], (16, PTS))
+    orders = first_order + lax.broadcasted_iota(jnp.int32, (16, 128), 0)
+    order_f = orders.astype(F32)
+    order_sq = order_f * order_f
+
+    def wide(x):
+        return jnp.concatenate([x] * (PTS // 128), axis=1)
+
+    start = wide(diag_ref[...]) + wide(order_f) * log_sine
+
+    def block(number, carry):
+        first, second, log_scale = carry
+        scale = jnp.exp(log_scale) * live
+        for position in range(16):
+            degree = number * 16 + position
+            lf = jnp.full((16, 128), degree, jnp.int32).astype(F32)
+            up = jnp.sqrt((4.0 * lf * lf - 1.0) / jnp.maximum(lf * lf - order_sq, 1.0))
+            lb = lf - 1.0
+            back = jnp.sqrt(
+                jnp.maximum(lb * lb - order_sq, 0.0) / jnp.maximum(4.0 * lb * lb - 1.0, 1.0)
+            )
+            up = jnp.where(degree > orders, up, 0.0)
+            onset = jnp.where(degree == orders, 1.0, 0.0)
+            current = wide(up) * (cosine * first - wide(back) * second) + wide(onset)
+            kept = jnp.where(jnp.full((16, PTS), degree, jnp.int32) <= LMAX, current * scale, 0.0)
+            for part in range(PTS // 128):
+                table[part, pl.ds(pl.multiple_of(degree * 16, 16), 16), :] = kept[
+                    :, part * 128 : part * 128 + 128
+                ]
+            second = first
+            first = current
+        magnitude = jnp.maximum(jnp.abs(first), jnp.abs(second))
+        factor = jnp.where(magnitude > 1.0, magnitude, 1.0)
+        return first / factor, second / factor, log_scale + jnp.log(factor)
+
+    zero = jnp.zeros((16, PTS), F32)
+    lax.fori_loop(0, 23, block, (zero, zero, start))
+    table[:, pl.ds(368 * 16, 16 * 16), :] = jnp.zeros((PTS // 128, 256, 128), F32)
+
+
+def legendre_tables(table, leg, legt):
+    def one(m, carry):
+        for part in range(PTS // 128):
+            lanes = slice(part * 128, part * 128 + 128)
+            values = table[part, pl.ds(m, DEG, stride=16), :]
+            leg[m, :, lanes] = values.astype(BF16)
+            legt[m, lanes, :] = values.T.astype(BF16)
+        return carry
+
+    lax.fori_loop(0, MDEV, one, 0)
 
 
 def window(row):
@@ -141,121 +128,236 @@
     return start // 128 * 128, start % 128
 
 
-def order_factor(first_ref):
-    order = first_ref[0] + pl.program_id(0)
-    edge = jnp.logical_or(order == 0, order == LMAX)
-    return jnp.where(edge, 1.0, 2.0)
+def enter():
+    band, member = lax.axis_index("space"), lax.axis_index("member")
+    barrier = pltpu.get_barrier_semaphore()
+
+    def signal(i, carry):
+        peer = lax.rem(band + i, BANDS)
+        pl.semaphore_signal(barrier, inc=1, device_id=(member, peer), device_id_type=MESH)
+        return carry
+
+    lax.fori_loop(1, BANDS, signal, 0)
+    pl.semaphore_wait(barrier, BANDS - 1)
+
+
+def send_group(source, target, group, sent, got):
+    band, member = lax.axis_index("space"), lax.axis_index("member")
+
+    def send(i, carry):
+        peer = lax.rem(band + i, BANDS)
+        pltpu.make_async_remote_copy(
+            src_ref=source.at[group, peer],
+            dst_ref=target.at[group, band],
+            send_sem=sent.at[group],
+            recv_sem=got.at[group],
+            device_id=(member, peer),
+            device_id_type=MESH,
+        ).start()
+        return carry
+
+    lax.fori_loop(1, BANDS, send, 0)
+    pltpu.make_async_copy(source.at[group, band], target.at[group, band], got.at[group]).start()
+
+
+def wait_arrived(source, target, group, got):
+    pltpu.make_async_copy(source.at[group], target.at[group], got.at[group]).wait()
+
+
+def wait_sent(source, target, group, sent):
+    most = pl.ds(0, BANDS - 1)
+    pltpu.make_async_copy(
+        source.at[group, most], target.at[group, most], sent.at[group]
+    ).wait()
+
+
+def gather_points(rows, points, order):
+    for r in range(BAND):
+        for k in range(2):
+            got = rows[r, pl.ds(k * GM + order, BANDS, stride=GK), :]
+            points[r * BANDS : (r + 1) * BANDS, k * 128 : (k + 1) * 128] = got.astype(BF16)
+
+
+def scatter_points(synth, made, order):
+    for r in range(BAND):
+        for k in range(2):
+            made[r, pl.ds(k * GM + order, BANDS, stride=GK), :] = synth[
+                r * BANDS : (r + 1) * BANDS, k * 128 : (k + 1) * 128
+            ]
+
+
+def order_factor(order):
+    return jnp.where(jnp.logical_or(order == 0, order == LMAX), 1.0, 2.0)
 
 
 def forward_kernel(
-    first_ref, z_ref, leg_ref, legt_ref, enc_ref, mix_ref, gain_ref, out_ref, rows, points, made
+    geo_ref, diag_ref, enc_ref, mix_ref, gain_ref, z_ref, out_ref, leg_out, legt_out,
+    table, leg, legt, arrived, rows, points, made, ready, sent_in, got_in, sent_out, got_out, kept
 ):
-    step = pl.program_id(0)
-
-    @pl.when(step == 0)
-    def _():
+    first_order = lax.axis_index("space") * MDEV
+    enter()
+    for group in range(GROUPS):
+        send_group(z_ref, arrived, group, sent_in, got_in)
+    legendre_rows(first_order, geo_ref, diag_ref, table)
+    legendre_tables(table, leg, legt)
+    save = pltpu.make_async_copy(leg, leg_out, kept.at[0])
+    save_t = pltpu.make_async_copy(legt, legt_out, kept.at[1])
+    save.start()
+    save_t.start()
+    points[...] = jnp.zeros((PTS, 256), BF16)
+
+    def one_group(group, carry):
+        wait_arrived(z_ref, arrived, group, got_in)
         for r in range(BAND):
             base, off = window(r)
-            pair = z_ref[:, base : base + 256].astype(F32)
+            pair = arrived[group, :, :, base : base + 256].astype(F32).reshape(BANDS * GK, 256)
             rows[r] = pltpu.roll(pair, (256 - off) % 256, 1)[:, :128]
-        points[...] = jnp.zeros((PTS, 256), BF16)
-
-    for r in range(BAND):
-        for k in range(2):
-            got = rows[r, pl.ds(k * MDEV + step, BANDS, stride=KM), :]
-            points[r * BANDS : (r + 1) * BANDS, k * 128 : (k + 1) * 128] = got.astype(BF16)
-    coeffs = dot(leg_ref[0], points[...], 1, 0).astype(BF16)
-    factor = order_factor(first_ref)
-    gain = gain_ref[...] * factor
-    filtered = []
-    for k in range(2):
-        channels = dot(coeffs[:, k * 128 : (k + 1) * 128], enc_ref[...], 1, 0).astype(BF16)
-        filtered.append((dot(channels, mix_ref[...], 1, 0) * gain).astype(BF16))
-    synth = dot(legt_ref[0], jnp.concatenate(filtered, axis=1), 1, 0)
-    for r in range(BAND):
-        for k in range(2):
-            made[r, pl.ds(k * MDEV + step, BANDS, stride=KM), :] = synth[
-                r * BANDS : (r + 1) * BANDS, k * 128 : (k + 1) * 128
-            ]
-
-    @pl.when(step == MDEV - 1)
-    def _():
+
+        def one_order(order, carry):
+            m = group * GM + order
+            gather_points(rows, points, order)
+            coeffs = dot(leg[m], points[...], 1, 0).astype(BF16)
+            gain = gain_ref[...] * order_factor(first_order + m)
+            filtered = []
+            for k in range(2):
+                channels = dot(coeffs[:, k * 128 : (k + 1) * 128], enc_ref[...], 1, 0).astype(BF16)
+                filtered.append((dot(channels, mix_ref[...], 1, 0) * gain).astype(BF16))
+            scatter_points(dot(legt[m], jnp.concatenate(filtered, axis=1), 1, 0), made, order)
+            return carry
+
+        lax.fori_loop(0, GM, one_order, 0)
         for r in range(BAND):
-            out_ref[:, r * CH : (r + 1) * CH] = made[r].astype(BF16)
+            ready[group, :, :, r * CH : (r + 1) * CH] = (
+                made[r].reshape(BANDS, GK, CH).astype(BF16)
+            )
+        send_group(ready, out_ref, group, sent_out, got_out)
+        return carry
+
+    lax.fori_loop(0, GROUPS, one_group, 0)
+    save.wait()
+    save_t.wait()
+    for group in range(GROUPS):
+        wait_sent(z_ref, arrived, group, sent_in)
+        wait_sent(ready, out_ref, group, sent_out)
+        wait_arrived(ready, out_ref, group, got_out)
 
 
 def backward_kernel(
-    first_ref, z_ref, leg_ref, legt_ref, enct_ref, mixt_ref, gain_ref, out_ref, rows, points, made
+    enct_ref, mixt_ref, gain_ref, leg_in, legt_in, z_ref, out_ref,
+    leg, legt, arrived, rows, points, made, ready, sent_in, got_in, sent_out, got_out, kept
 ):
-    step = pl.program_id(0)
-
-    @pl.when(step == 0)
-    def _():
+    first_order = lax.axis_index("space") * MDEV
+    load = pltpu.make_async_copy(leg_in, leg, kept.at[0])
+    load_t = pltpu.make_async_copy(legt_in, legt, kept.at[1])
+    load.start()
+    load_t.start()
+    enter()
+    for group in range(GROUPS):
+        send_group(z_ref, arrived, group, sent_in, got_in)
+    points[...] = jnp.zeros((PTS, 256), BF16)
+    load.wait()
+    load_t.wait()
+
+    def one_group(group, carry):
+        wait_arrived(z_ref, arrived, group, got_in)
         for r in range(BAND):
-            rows[r] = z_ref[:, r * CH : (r + 1) * CH].astype(F32)
-        points[...] = jnp.zeros((PTS, 256), BF16)
-
-    for r in range(BAND):
-        for k in range(2):
-            got = rows[r, pl.ds(k * MDEV + step, BANDS, stride=KM), :]
-            points[r * BANDS : (r + 1) * BANDS, k * 128 : (k + 1) * 128] = got.astype(BF16)
-    grads = dot(leg_ref[0], points[...], 1, 0)
-    gain = gain_ref[...] * order_factor(first_ref)
-    back = []
-    for k in range(2):
-        scaled = (grads[:, k * 128 : (k + 1) * 128] * gain).astype(BF16)
-        channels = dot(scaled, mixt_ref[...], 1, 0).astype(BF16)
-        back.append(dot(channels, enct_ref[...], 1, 0).astype(BF16))
-    synth = dot(legt_ref[0], jnp.concatenate(back, axis=1), 1, 0)
-    for r in range(BAND):
-        for k in range(2):
-            made[r, pl.ds(k * MDEV + step, BANDS, stride=KM), :] = synth[
-                r * BANDS : (r + 1) * BANDS, k * 128 : (k + 1) * 128
-            ]
-
-    @pl.when(step == MDEV - 1)
-    def _():
-        low = jnp.zeros((BANDS * KM, 128), F32)
+            rows[r] = (
+                arrived[group, :, :, r * CH : (r + 1) * CH].astype(F32).reshape(BANDS * GK, CH)
+            )
+
+        def one_order(order, carry):
+            m = group * GM + order
+            gather_points(rows, points, order)
+            grads = dot(leg[m], points[...], 1, 0)
+            gain = gain_ref[...] * order_factor(first_order + m)
+            back = []
+            for k in range(2):
+                scaled = (grads[:, k * 128 : (k + 1) * 128] * gain).astype(BF16)
+                channels = dot(scaled, mixt_ref[...], 1, 0).astype(BF16)
+                back.append(dot(channels, enct_ref[...], 1, 0).astype(BF16))
+            scatter_points(dot(legt[m], jnp.concatenate(back, axis=1), 1, 0), made, order)
+            return carry
+
+        lax.fori_loop(0, GM, one_order, 0)
+
+        def put(at, value):
+            ready[group, :, :, at : at + 128] = value.reshape(BANDS, GK, 128).astype(BF16)
+
+        low = spill = jnp.zeros((BANDS * GK, 128), F32)
         at = 0
         for r in range(BAND):
             base, off = window(r)
             while at < base:
-                out_ref[:, at : at + 128] = low.astype(BF16)
+                put(at, low)
                 low = spill
                 at += 128
             value = made[r]
-            pair = jnp.concatenate([value, jnp.zeros_like(value)], axis=1)
-            moved = pltpu.roll(pair, off, 1)
+            moved = pltpu.roll(jnp.concatenate([value, jnp.zeros_like(value)], axis=1), off, 1)
             low = low + moved[:, :128]
             spill = moved[:, 128:]
-        out_ref[:, at : at + 128] = low.astype(BF16)
-        at += 128
-        out_ref[:, at : at + 128] = spill.astype(BF16)
-
-
-def spectral(kernel, lanes_out, first_order, z, leg, legt, first_w, second_w, gain):
+        put(at, low)
+        put(at + 128, spill)
+        send_group(ready, out_ref, group, sent_out, got_out)
+        return carry
+
+    lax.fori_loop(0, GROUPS, one_group, 0)
+    for group in range(GROUPS):
+        wait_sent(z_ref, arrived, group, sent_in)
+        wait_sent(ready, out_ref, group, sent_out)
+        wait_arrived(ready, out_ref, group, got_out)
+
+
+VMEM = pl.BlockSpec(memory_space=pltpu.VMEM)
+ANY = pl.BlockSpec(memory_space=pl.ANY)
+LEG = jax.ShapeDtypeStruct((MDEV, DEG, PTS), BF16)
+LEGT = jax.ShapeDtypeStruct((MDEV, PTS, DEG), BF16)
+
+
+def chunks(lanes):
+    return (GROUPS, BANDS, GK, lanes)
+
+
+def spectral_scratch(lanes_in, lanes_out):
+    return [
+        pltpu.VMEM(LEG.shape, BF16),
+        pltpu.VMEM(LEGT.shape, BF16),
+        pltpu.VMEM(chunks(lanes_in), BF16),
+        pltpu.VMEM((BAND, BANDS * GK, 128), F32),
+        pltpu.VMEM((PTS, 256), BF16),
+        pltpu.VMEM((BAND, BANDS * GK, 128), F32),
+        pltpu.VMEM(chunks(lanes_out), BF16),
+    ] + [pltpu.SemaphoreType.DMA((GROUPS,))] * 4 + [pltpu.SemaphoreType.DMA((2,))]
+
+
+def remote_params(collective):
+    return pltpu.CompilerParams(
+        collective_id=collective, vmem_limit_bytes=58 * 1024 * 1024, has_side_effects=True
+    )
+
+
+def forward(geo, diag, enc, mix, gain, z):
     return pl.pallas_call(
-        kernel,
-        grid=(MDEV,),
-        in_specs=[
-            SMEM,
-            whole(z.shape),
-            pl.BlockSpec((1, DEG, PTS), lambda m: (m, 0, 0)),
-            pl.BlockSpec((1, PTS, DEG), lambda m: (m, 0, 0)),
-            whole((128, 128)),
-            whole((128, 128)),
-            whole((DEG, CH)),
-        ],
-        out_specs=whole((BANDS * KM, lanes_out)),
-        out_shape=jax.ShapeDtypeStruct((BANDS * KM, lanes_out), BF16),
-        scratch_shapes=[
-            pltpu.VMEM((BAND, BANDS * KM, 128), F32),
-            pltpu.VMEM((PTS, 256), BF16),
-            pltpu.VMEM((BAND, BANDS * KM, 128), F32),
-        ],
-        compiler_params=params(),
-        name=kernel.__name__,
-    )(first_order, z, leg, legt, first_w, second_w, gain)
+        forward_kernel,
+        in_specs=[VMEM] * 6,
+        out_specs=[ANY] * 3,
+        out_shape=[jax.ShapeDtypeStruct(chunks(WIDE), BF16), LEG, LEGT],
+        scratch_shapes=[pltpu.VMEM((PTS // 128, DEG * 16, 128), F32)]
+        + spectral_scratch(FLAT, WIDE),
+        compiler_params=remote_params(1),
+        name="forward",
+    )(geo, diag, enc, mix, gain, z)
+
+
+def backward(enct, mixt, gain, leg, legt, z):
+    return pl.pallas_call(
+        backward_kernel,
+        in_specs=[VMEM] * 3 + [ANY] * 2 + [VMEM],
+        out_specs=ANY,
+        out_shape=jax.ShapeDtypeStruct(chunks(FLAT), BF16),
+        scratch_shapes=spectral_scratch(WIDE, FLAT),
+        compiler_params=remote_params(2),
+        name="backward",
+    )(enct, mixt, gain, leg, legt, z)
 
 
 def grid_kernel(live_ref, s_ref, c_ref, x_ref, enct_ref, dect_ref, pred_ref, slope_ref):
@@ -412,7 +514,6 @@
     own_sine = jnp.sin(own_lat)
     own_weight = own_live * own_sine * (math.pi / (NLAT - 1) / NLON)
     own_area = 8.0 * own_sine * own_live
-    first_order = first.reshape(1)
 
     c = fourier_table()
     diag = lax.dynamic_slice_in_dim(jnp.asarray(diagonal_logs()), first, 16)
@@ -433,12 +534,8 @@
         jnp.einsum("aj,bj->ab", c, flat, preferred_element_type=F32) * lane_weight[None]
     ).astype(BF16)
 
-    arrived = exchange(zonal, "space")
-    leg, legt = legendre(first_order, geo, diag)
-    synth = spectral(
-        forward_kernel, WIDE, first_order, arrived, leg, legt, enc_wide, mixing_weight, gain
-    )
-    synth = exchange(synth, "space")
+    synth, leg, legt = forward(geo, diag, enc_wide, mixing_weight, gain, zonal.reshape(chunks(FLAT)))
+    synth = synth.reshape(BANDS * KM, WIDE)
     predicted, slope = grid_stage(own_live, synth, c, x, enct, dect)
 
     everyone = exchange(predicted, "member").reshape(MEMBERS, 2, FIELDS, NLON)
@@ -448,11 +545,9 @@
     share = score_stage(area, everyone, truth)
     score = exchange(share.reshape(16, FIELDS, NLON), "member")
 
-    grads = exchange(grad_stage(score, slope, c, dec), "space")
-    grads = spectral(
-        backward_kernel, FLAT, first_order, grads, leg, legt, enct_wide, mixing_weight.T, gain
-    )
-    grads = exchange(grads, "space")
+    grads = grad_stage(score, slope, c, dec).reshape(chunks(WIDE))
+    grads = backward(enct_wide, mixing_weight.T, gain, leg, legt, grads)
+    grads = grads.reshape(BANDS * KM, FLAT)
     result = final_stage(own_weight, own_live, grads, c, score, dec, enc)
     prediction = jnp.transpose(predicted[:BAND], (1, 0, 2))[None]
     return (prediction, jnp.transpose(result, (1, 0, 2))[None])

time: 408 us -> 347 us (0.85)
  waiting for transfers between devices: 239 us -> 37.4 us
  Pallas kernels: 90.2 us -> 261 us
  starting transfers between devices: 37.6 us -> 10.4 us
    all_to_all x6 -> x2, waiting for transfers between devices: 239 us -> 37.4 us  [exchange(): return lax.all_to_all(array, axis, split_axis=0, concat_axis=0, tiled=True)]
    pallas_call x3 -> x2, Pallas kernels: 53.5 us -> 224 us  [the longest x1 114 us: forward(): pl.pallas_call(forward_kernel, in_specs=[VMEM] * 6, out_specs=[ANY] * 3,...]
    all_to_all x6 -> x2, starting transfers between devices: 37.6 us -> 10.4 us  [exchange(): return lax.all_to_all(array, axis, split_axis=0, concat_axis=0, tiled=True)]
    unnamed x40 -> x28, local copies, waits for them, and re-layouts: 19.2 us -> 15.3 us
  transfers between devices with their start and end apart: 6 -> 2, of which waited for: 6 -> 2; matrix products, arithmetic and copies ran while one was open for 4% -> 4% of each run, Pallas kernels for 4% -> 0%
where the time goes in v2:
time: 347 us; the launch traced here: 345 us
  Pallas kernels  261 us (75%)
  waiting for transfers between devices  37.4 us (11%)
  local copies, waits for them, and re-layouts  25.2 us (7%)
  starting transfers between devices  10.4 us (3%)
  other arithmetic  5.88 us (2%)
  matrix products  4.39 us (1%)
    pallas_call x1, Pallas kernels, forward(): pl.pallas_call(forward_kernel, in_specs=[VMEM] * 6, out_specs=[ANY] * 3,...  114 us
    pallas_call x1, Pallas kernels, backward(): pl.pallas_call(backward_kernel, in_specs=[VMEM] * 3 + [ANY] * 2 + [VMEM],...  110 us
    all_to_all x2, waiting for transfers between devices, exchange(): return lax.all_to_all(array, axis, split_axis=0, concat_axis=0, tiled=True)  37.4 us
    unnamed x28, local copies, waits for them, and re-layouts  15.3 us
    all_to_all x2, starting transfers between devices, exchange(): return lax.all_to_all(array, axis, split_axis=0, concat_axis=0, tiled=True)  10.4 us
    pallas_call x1, Pallas kernels, grid_stage(): pl.pallas_call(grid_kernel, grid=(5,), in_specs=[SMEM, pl.BlockSpec((BAND...  10.2 us
    pallas_call x1, Pallas kernels, score_stage(): pl.pallas_call(score_kernel, grid=(2, 6), in_specs=[SMEM, pl.BlockSpec((M...  10.1 us
    pallas_call x1, Pallas kernels, grad_stage(): pl.pallas_call(grad_kernel, grid=(5,), in_specs=[pl.BlockSpec((3, FIELDS,...  8.27 us
  transfers between devices with their start and end apart: 2, of which 2 were waited for; matrix products, arithmetic and copies ran while one was open for 4% of the time, Pallas kernels for 0%

profile of v2, /device:TPU:7, one launch (start us, length us, event | category | flops | bytes accessed | tf_op | source)
XLA Modules:
  0.0 344.8 jit_solution(7928820326952572480)
XLA Ops:
  0.7 1.3 fusion.10
  2.0 1.1 fusion.11.live_ref
  3.1 0.7 select_reduce_fusion.1
  3.9 0.1 maximum_log_fusion
  4.0 0.8 copy.31
  4.8 0.0 copy-start.4
  4.8 0.1 copy.42
  4.9 1.2 select_multiply_fusion.weight_ref
  6.2 0.0 copy-start.9
  6.2 2.0 copy.43
  8.2 0.0 copy-done.4
  8.2 0.0 copy-start.1
  8.3 0.0 copy-start.6
  8.3 0.0 copy-start.2
  8.3 2.0 reshape.140
  10.3 0.8 dynamic_slice.9
  11.0 0.6 pad.16.clone.enc_ref
  11.7 0.0 copy-done.6
  11.7 0.7 pad.17.gain_ref
  12.3 0.0 copy-done.9
  12.3 0.0 copy-done.1
  12.3 0.1 select_reduce_fusion
  12.4 0.0 copy-done.2
  12.4 4.4 %fusion = bf16[1152,768]{0,1:T(8,128)(2,1)} fusion(bf16[768,720]{1,0:T(8,128)(2,1)S(1)} %copy-done.2, f32[1152]{0:T(1024)S(1)} %select_reduce_fusion, bf16[1095,720]{1,0:T(8,128)(2,1)} %reshape.140), kind=kOutput, calls=%fused_computation.1 | convolution fusion | flops 1275789312 | bytes 4456800 | tf_op jit(solution)/shard_map/aj,bj->ab/dot_general | solution.py:534
  16.9 0.6 stack.10.geo_ref
  17.5 0.7 broadcast_in_dim.58.diag_ref
  18.2 113.7 %forward.1 = (bf16[3,32,8,1920]{3,2,1,0:T(8,128)(2,1)}, bf16[12,384,512]{2,1,0:T(8,128)(2,1)}, bf16[12,512,384]{2,1,0:T(8,128)(2,1)}) custom-call(f32[8,512]{1,0:T(8,128)} %stack.10.geo_ref, f32[16,128]{1,0:T(8,128)} %broadcast_in_dim.58.diag_ref, bf16[128,128]{1,0:T(8,128)(2,1)} %pad.16.clone.enc_ref, bf16[128,128]{1,0:T(8,128)(2,1)} %mix_ref.1, ...), custom_call_target="tpu_custom_call" | custom-call | tf_op jit(solution)/shard_map/forward/pallas_call | solution.py:339
  131.9 10.2 %grid_stage.1 = (bf16[16,73,720]{2,1,0:T(8,128)(2,1)}, bf16[15,128,720]{2,1,0:T(8,128)(2,1)}) custom-call(f32[16]{0:T(128)} %fusion.11.live_ref, bf16[768,1920]{1,0:T(8,128)(2,1)} %bitcast.37, bf16[768,720]{1,0:T(8,128)(2,1)} %constant.86.clone.c_ref, bf16[15,73,720]{2,1,0:T(8,128)(2,1)} %bitcast.31, bf16[128,73]{1,0:T(8,128)(2,1)} %bitcast.39, ...), custom_call_target="tpu_custom_call" | custom-call | tf_op jit(solution)/shard_map/grid_stage/pallas_call | solution.py:380
  142.1 5.8 %all-to-all-start = ((bf16[16,73,720]{2,1,0:T(8,128)(2,1)}), bf16[16,73,720]{2,1,0:T(8,128)(2,1)S(1)}, u32[]{:S(2)}, u32[]{:S(2)}) async-start(bf16[16,73,720]{2,1,0:T(8,128)(2,1)} %get-tuple-element.8), calls=%async_computation | async-start | bytes 3932160 | tf_op jit(solution)/shard_map/all_to_all | solution.py:489
  147.9 3.3 copy.36
  151.2 1.2 multiply_select_fusion
  152.4 0.6 dynamic_slice.10.area_ref
  153.0 1.7 fusion.2.o_ref
  154.7 18.0 %all-to-all-done = bf16[16,73,720]{2,1,0:T(8,128)(2,1)S(1)} async-done(((bf16[16,73,720]{2,1,0:T(8,128)(2,1)}), bf16[16,73,720]{2,1,0:T(8,128)(2,1)S(1)}, u32[]{:S(2)}, u32[]{:S(2)}) %all-to-all-start) | async-done | bytes 1681952 | tf_op jit(solution)/shard_map/all_to_all | solution.py:489
  172.7 0.0 copy-start.3
  172.7 1.3 copy-done.3
  174.0 10.1 %score_stage.1 = bf16[8,2,73,720]{3,2,1,0:T(8,128)(2,1)} custom-call(f32[2]{0:T(128)} %dynamic_slice.10.area_ref, bf16[8,2,73,720]{3,2,1,0:T(8,128)(2,1)} %bitcast.33, bf16[2,73,720]{2,1,0:T(8,128)(2,1)} %fusion.2.o_ref), custom_call_target="tpu_custom_call" | custom-call | tf_op jit(solution)/shard_map/score_stage/pallas_call | solution.py:426
  184.1 0.0 copy-start.7
  184.1 0.0 copy-start.8
  184.1 4.6 %all-to-all-start.1 = ((bf16[16,73,720]{2,1,0:T(8,128)(2,1)}), bf16[16,73,720]{2,1,0:T(8,128)(2,1)S(1)}, u32[]{:S(2)}, u32[]{:S(2)}) async-start(bf16[16,73,720]{2,1,0:T(8,128)(2,1)} %bitcast.34), calls=%async_computation.1 | async-start | bytes 3932160 | tf_op jit(solution)/shard_map/all_to_all | solution.py:489
  188.7 0.0 copy-done.7
  188.7 0.7 copy.35
  189.4 0.0 copy-done.8
  189.4 0.7 copy.37.dec_ref
  190.1 1.6 slice_bitcast_fusion
  191.8 0.0 copy-start.5
  191.8 1.8 copy.39
  193.5 0.0 copy-done.5
  193.5 0.6 pad_bitcast_fusion.enct_ref
  194.2 19.4 %all-to-all-done.1.g_ref = bf16[16,73,720]{2,1,0:T(8,128)(2,1)S(1)} async-done(((bf16[16,73,720]{2,1,0:T(8,128)(2,1)}), bf16[16,73,720]{2,1,0:T(8,128)(2,1)S(1)}, u32[]{:S(2)}, u32[]{:S(2)}) %all-to-all-start.1) | async-done | bytes 1681952 | tf_op jit(solution)/shard_map/all_to_all | solution.py:489
  213.5 0.0 copy-start
  213.5 1.3 copy-done
  214.8 8.3 %grad_stage.1 = bf16[768,1920]{1,0:T(8,128)(2,1)} custom-call(bf16[16,73,720]{2,1,0:T(8,128)(2,1)} %copy-done, bf16[15,128,720]{2,1,0:T(8,128)(2,1)} %get-tuple-element.11.slope_ref, bf16[768,720]{1,0:T(8,128)(2,1)} %constant.86.clone.c_ref, bf16[128,73]{1,0:T(8,128)(2,1)} %copy.37.dec_ref), custom_call_target="tpu_custom_call" | custom-call | tf_op jit(solution)/shard_map/grad_stage/pallas_call | solution.py:450
  223.1 110.3 %backward.1 = bf16[3,32,8,1152]{3,2,1,0:T(8,128)(2,1)} custom-call(bf16[128,128]{1,0:T(8,128)(2,1)} %pad_bitcast_fusion.enct_ref, bf16[128,128]{1,0:T(8,128)(2,1)} %bitcast.40, f32[384,128]{1,0:T(8,128)} %pad.17.gain_ref, bf16[12,384,512]{2,1,0:T(8,128)(2,1)} %get-tuple-element.9.leg_in, bf16[12,512,384]{2,1,0:T(8,128)(2,1)} %get-tuple-element.10.legt_in, ...), custom_call_target="tpu_custom_call" | custom-call | tf_op jit(solution)/shard_map/backward/pallas_call | solution.py:352
  333.4 8.2 %final_stage.1 = bf16[15,73,720]{2,1,0:T(8,128)(2,1)} custom-call(f32[16]{0:T(128)} %copy-done.9, f32[16]{0:T(128)} %fusion.11.live_ref, bf16[768,1152]{1,0:T(8,128)(2,1)} %bitcast.36, bf16[768,720]{1,0:T(8,128)(2,1)} %constant.86.clone.c_ref, bf16[16,73,720]{2,1,0:T(8,128)(2,1)} %copy-done, bf16[128,73]{1,0:T(8,128)(2,1)} %copy.37.dec_ref, ...), custom_call_target="tpu_custom_call" | custom-call | tf_op jit(solution)/shard_map/final_stage/pallas_call | solution.py:477
  341.6 3.3 copy.40
  (5 shorter events, 0.0 us)
Async XLA Ops:
  4.8 3.4 copy-start.4
  6.2 6.2 %copy-start.9 = (f32[16]{0:T(128)}, f32[16]{0:T(128)S(1)}, u32[]{:S(2)}) copy-start(f32[16]{0:T(128)S(1)} %select_multiply_fusion.weight_ref) | copy-start | bytes 196
  8.2 4.1 %copy-start.1 = (bf16[1,73,15,720]{3,1,2,0:T(8,128)(2,1)}, bf16[1,73,15,720]{3,1,2,0:T(8,128)(2,1)S(1)}, u32[]{:S(2)}) copy-start(bf16[1,73,15,720]{3,1,2,0:T(8,128)(2,1)S(1)} %copy.43) | copy-start | bytes 4730404
  8.3 3.4 copy-start.6
  8.3 4.2 %copy-start.2 = (bf16[768,720]{1,0:T(8,128)(2,1)S(1)}, bf16[768,720]{1,0:T(8,128)(2,1)}, u32[]{:S(2)}) copy-start(bf16[768,720]{1,0:T(8,128)(2,1)} %constant.86.clone.c_ref) | copy-start | bytes 3317764
  142.1 30.6 %all-to-all-start = ((bf16[16,73,720]{2,1,0:T(8,128)(2,1)}), bf16[16,73,720]{2,1,0:T(8,128)(2,1)S(1)}, u32[]{:S(2)}, u32[]{:S(2)}) async-start(bf16[16,73,720]{2,1,0:T(8,128)(2,1)} %get-tuple-element.8), calls=%async_computation | async-start | bytes 3932160 | tf_op jit(solution)/shard_map/all_to_all | solution.py:489
  172.7 1.3 copy-start.3
  184.1 4.6 %copy-start.7 = (bf16[128,128]{1,0:T(8,128)(2,1)S(1)}, bf16[128,128]{1,0:T(8,128)(2,1)}, u32[]{:S(2)}) copy-start(bf16[128,128]{1,0:T(8,128)(2,1)} %mix_ref.1) | copy-start | bytes 98308
  184.1 5.3 %copy-start.8 = (bf16[128,73]{0,1:T(8,128)(2,1)S(1)}, bf16[128,73]{0,1:T(8,128)(2,1)}, u32[]{:S(2)}) copy-start(bf16[128,73]{0,1:T(8,128)(2,1)} %param.15) | copy-start | bytes 56068
  184.1 29.4 %all-to-all-start.1 = ((bf16[16,73,720]{2,1,0:T(8,128)(2,1)}), bf16[16,73,720]{2,1,0:T(8,128)(2,1)S(1)}, u32[]{:S(2)}, u32[]{:S(2)}) async-start(bf16[16,73,720]{2,1,0:T(8,128)(2,1)} %bitcast.34), calls=%async_computation.1 | async-start | bytes 3932160 | tf_op jit(solution)/shard_map/all_to_all | solution.py:489
  191.8 1.8 copy-start.5
  213.5 1.3 copy-start

commit v3 on v2

--- a/solution.py
+++ b/solution.py
@@ -1,4 +1,3 @@
-import functools
 import math
 
 import jax
@@ -35,16 +34,6 @@
 
 def dot(a, b, ca, cb):
     return lax.dot_general(a, b, (((ca,), (cb,)), ((), ())), preferred_element_type=F32)
-
-
-def params(mb=56):
-    return pltpu.CompilerParams(
-        vmem_limit_bytes=mb * 1024 * 1024, dimension_semantics=("arbitrary",)
-    )
-
-
-def whole(shape):
-    return pl.BlockSpec(shape, lambda *g: (0,) * len(shape))
 
 
 SMEM = pl.BlockSpec(memory_space=pltpu.SMEM)
@@ -360,51 +349,12 @@
     )(enct, mixt, gain, leg, legt, z)
 
 
-def grid_kernel(live_ref, s_ref, c_ref, x_ref, enct_ref, dect_ref, pred_ref, slope_ref):
-    step = pl.program_id(0)
-    for part in range(3):
-        lanes = slice(part * CH, (part + 1) * CH)
-        field = dot(s_ref[:, lanes], c_ref[...], 0, 0)
-        live = live_ref[step * 3 + part]
-        state = x_ref[part]
-        hidden = (dot(enct_ref[...], state, 1, 0) * live).astype(BF16).astype(F32)
-        cdf = 0.5 * (1.0 + lax.erf(field * (1.0 / math.sqrt(2.0))))
-        slope = cdf + field * jnp.exp(-0.5 * field * field) * (1.0 / math.sqrt(2.0 * math.pi))
-        block = ((field * cdf + hidden) * live).astype(BF16)
-        decoded = dot(dect_ref[...], block, 1, 0)
-        pred_ref[part] = ((state.astype(F32) + decoded) * live).astype(BF16)
-        slope_ref[part] = slope.astype(BF16)
-
-
-def grid_stage(live, s, c, x, enct, dect):
-    return pl.pallas_call(
-        grid_kernel,
-        grid=(5,),
-        in_specs=[
-            SMEM,
-            pl.BlockSpec((BANDS * KM, 3 * CH), lambda g: (0, g)),
-            whole((BANDS * KM, NLON)),
-            pl.BlockSpec((3, FIELDS, NLON), lambda g: (g, 0, 0)),
-            whole((CH, FIELDS)),
-            whole((FIELDS, CH)),
-        ],
-        out_specs=[
-            pl.BlockSpec((3, FIELDS, NLON), lambda g: (g, 0, 0)),
-            pl.BlockSpec((3, CH, NLON), lambda g: (g, 0, 0)),
-        ],
-        out_shape=[
-            jax.ShapeDtypeStruct((16, FIELDS, NLON), BF16),
-            jax.ShapeDtypeStruct((BAND, CH, NLON), BF16),
-        ],
-        compiler_params=params(),
-        name="grid_stage",
-    )(live, s, c, x, enct, dect)
-
-
-def score_kernel(area_ref, p_ref, o_ref, out_ref):
-    area = area_ref[pl.program_id(0)]
-    values = [p_ref[e, 0].astype(F32) for e in range(MEMBERS)]
-    truth = o_ref[0].astype(F32)
+TILES = [(t * 128, min(128, NLON - t * 128)) for t in range(6)]
+
+
+def score_tile(p_ref, o_ref, out_ref, group, lanes, area):
+    values = [p_ref[group, e, :, lanes].astype(F32) for e in range(MEMBERS)]
+    truth = o_ref[group, :, lanes].astype(F32)
 
     def inverse(gap):
         return lax.rsqrt(jnp.sum(gap * gap, axis=0, keepdims=True) + EPSILON)
@@ -419,54 +369,141 @@
         for f in range(MEMBERS):
             if f != e:
                 total = total - (values[e] - values[f]) * weights[e, f]
-        out_ref[e, 0] = total.astype(BF16)
-
-
-def score_stage(area, everyone, truth):
+        out_ref[group, e, :, lanes] = total.astype(BF16)
+
+
+def middle_kernel(
+    live_ref, area_ref, s_ref, c_ref, x_ref, o_ref, enct_ref, dect_ref, dec_ref,
+    pred_ref, score_ref, out_ref,
+    mine, everyone, share, slope, wide_rows, sent_in, got_in, sent_out, got_out,
+):
+    band, member = lax.axis_index("space"), lax.axis_index("member")
+    barrier = pltpu.get_barrier_semaphore()
+    for i in range(1, MEMBERS):
+        peer = lax.rem(member + i, MEMBERS)
+        pl.semaphore_signal(barrier, inc=1, device_id=(peer, band), device_id_type=MESH)
+    pl.semaphore_wait(barrier, MEMBERS - 1)
+
+    def send(source, target, group, peer, sent, got):
+        pltpu.make_async_remote_copy(
+            src_ref=source.at[group, peer],
+            dst_ref=target.at[group, member],
+            send_sem=sent.at[group],
+            recv_sem=got.at[group],
+            device_id=(peer, band),
+            device_id_type=MESH,
+        ).start()
+
+    def keep(source, target, group, got):
+        pltpu.make_async_copy(
+            source.at[group, member], target.at[group, member], got.at[group]
+        ).start()
+
+    def one_row(group, peer):
+        row = 2 * peer + group
+        held = jnp.minimum(row, BAND - 1)
+        lanes = pl.ds(pl.multiple_of(held * CH, CH), CH)
+        field = dot(s_ref[:, lanes], c_ref[...], 0, 0)
+        live = live_ref[row]
+        state = x_ref[held]
+        hidden = (dot(enct_ref[...], state, 1, 0) * live).astype(BF16).astype(F32)
+        cdf = 0.5 * (1.0 + lax.erf(field * (1.0 / math.sqrt(2.0))))
+        gradient = cdf + field * jnp.exp(-0.5 * field * field) * (1.0 / math.sqrt(2.0 * math.pi))
+        block = ((field * cdf + hidden) * live).astype(BF16)
+        decoded = dot(dect_ref[...], block, 1, 0)
+        result = (state.astype(F32) + decoded) * live
+        mine[group, peer] = result.astype(BF16)
+        slope[group, peer] = gradient.astype(BF16)
+        for t, (start, size) in enumerate(TILES):
+            wide_rows[t, pl.ds(row, FIELDS, stride=16), :size] = result[:, start : start + size]
+
+    for group in range(2):
+
+        def one_peer(i, carry):
+            peer = lax.rem(member + i, MEMBERS)
+            one_row(group, peer)
+            send(mine, everyone, group, peer, sent_in, got_in)
+            return carry
+
+        lax.fori_loop(1, MEMBERS, one_peer, 0)
+        one_row(group, member)
+        keep(mine, everyone, group, got_in)
+
+    for t, (start, size) in enumerate(TILES):
+        rows = wide_rows[t].reshape(FIELDS, 16, 128)
+        pred_ref[:, :, start : start + size] = rows[:, :BAND, :size].astype(BF16)
+
+    def score_group(group, carry):
+        pltpu.make_async_copy(mine.at[group], everyone.at[group], got_in.at[group]).wait()
+        area = area_ref[2 * member + group]
+
+        def one_tile(t, inner):
+            lanes = pl.ds(pl.multiple_of(t * 128, 128), 128)
+            score_tile(everyone, o_ref, share, group, lanes, area)
+            return inner
+
+        lax.fori_loop(0, 5, one_tile, 0)
+        score_tile(everyone, o_ref, share, group, pl.ds(640, NLON - 640), area)
+
+        def one_peer(i, inner):
+            send(share, score_ref, group, lax.rem(member + i, MEMBERS), sent_out, got_out)
+            return inner
+
+        lax.fori_loop(1, MEMBERS, one_peer, 0)
+        keep(share, score_ref, group, got_out)
+        return carry
+
+    lax.fori_loop(0, 2, score_group, 0)
+
+    for group in range(2):
+        pltpu.make_async_copy(share.at[group], score_ref.at[group], got_out.at[group]).wait()
+        for first in range(0, MEMBERS, 2):
+            fields = []
+            for peer in (first, first + 1):
+                block = dot(dec_ref[...], score_ref[group, peer], 1, 0)
+                fields.append((block * slope[group, peer].astype(F32)).astype(BF16))
+            made = dot(c_ref[...], jnp.concatenate(fields, axis=0), 1, 1).astype(BF16)
+            for part in range(2):
+                row = 2 * (first + part) + group
+                if row < BAND:
+                    out_ref[:, row * CH : (row + 1) * CH] = made[:, part * CH : (part + 1) * CH]
+
+    most = pl.ds(0, MEMBERS - 1)
+    for group in range(2):
+        for source, target, sent in ((mine, everyone, sent_in), (share, score_ref, sent_out)):
+            pltpu.make_async_copy(
+                source.at[group, most], target.at[group, most], sent.at[group]
+            ).wait()
+
+
+def middle(live, area, s, c, x, truth, enct, dect, dec):
+    quarter = (2, MEMBERS, FIELDS, NLON)
     return pl.pallas_call(
-        score_kernel,
-        grid=(2, 6),
-        in_specs=[
-            SMEM,
-            pl.BlockSpec((MEMBERS, 1, FIELDS, 128), lambda r, j: (0, r, 0, j)),
-            pl.BlockSpec((1, FIELDS, 128), lambda r, j: (r, 0, j)),
+        middle_kernel,
+        in_specs=[SMEM] * 2 + [VMEM] * 7,
+        out_specs=[VMEM] * 3,
+        out_shape=[
+            jax.ShapeDtypeStruct((FIELDS, BAND, NLON), BF16),
+            jax.ShapeDtypeStruct(quarter, BF16),
+            jax.ShapeDtypeStruct((BANDS * KM, WIDE), BF16),
         ],
-        out_specs=pl.BlockSpec((MEMBERS, 1, FIELDS, 128), lambda r, j: (0, r, 0, j)),
-        out_shape=jax.ShapeDtypeStruct((MEMBERS, 2, FIELDS, NLON), BF16),
-        compiler_params=pltpu.CompilerParams(dimension_semantics=("arbitrary", "arbitrary")),
-        name="score_stage",
-    )(area, everyone, truth)
-
-
-def grad_kernel(g_ref, slope_ref, c_ref, dec_ref, out_ref):
-    fields = []
-    for part in range(3):
-        block = dot(dec_ref[...], g_ref[part], 1, 0)
-        fields.append((block * slope_ref[part].astype(F32)).astype(BF16))
-    out_ref[...] = dot(c_ref[...], jnp.concatenate(fields, axis=0), 1, 1).astype(BF16)
-
-
-def grad_stage(score, slope, c, dec):
-    return pl.pallas_call(
-        grad_kernel,
-        grid=(5,),
-        in_specs=[
-            pl.BlockSpec((3, FIELDS, NLON), lambda g: (g, 0, 0)),
-            pl.BlockSpec((3, CH, NLON), lambda g: (g, 0, 0)),
-            whole((BANDS * KM, NLON)),
-            whole((CH, FIELDS)),
-        ],
-        out_specs=pl.BlockSpec((BANDS * KM, 3 * CH), lambda g: (0, g)),
-        out_shape=jax.ShapeDtypeStruct((BANDS * KM, WIDE), BF16),
-        compiler_params=params(),
-        name="grad_stage",
-    )(score, slope, c, dec)
+        scratch_shapes=[
+            pltpu.VMEM(quarter, BF16),
+            pltpu.VMEM(quarter, BF16),
+            pltpu.VMEM(quarter, BF16),
+            pltpu.VMEM((2, MEMBERS, CH, NLON), BF16),
+            pltpu.VMEM((len(TILES), FIELDS * 16, 128), F32),
+        ]
+        + [pltpu.SemaphoreType.DMA((2,))] * 4,
+        compiler_params=remote_params(3),
+        name="middle",
+    )(live, area, s, c, x, truth, enct, dect, dec)
 
 
 def final_kernel(weight_ref, live_ref, z_ref, c_ref, g_ref, dec_ref, enc_ref, out_ref, spread):
     spread[...] = dot(z_ref[...], c_ref[...], 0, 0)
     for r in range(BAND):
-        score = g_ref[r]
+        score = g_ref[r % 2, r // 2]
         block = dot(dec_ref[...], score, 1, 0).astype(BF16)
         local = dot(enc_ref[...], block, 1, 0)
         far = spread[r * FIELDS : (r + 1) * FIELDS, :] * weight_ref[r]
@@ -483,10 +520,6 @@
         compiler_params=pltpu.CompilerParams(vmem_limit_bytes=56 * 1024 * 1024),
         name="final_stage",
     )(weight, live, z, c, score, dec, enc)
-
-
-def exchange(array, axis):
-    return lax.all_to_all(array, axis, split_axis=0, concat_axis=0, tiled=True)
 
 
 def on_device(
@@ -536,21 +569,16 @@
 
     synth, leg, legt = forward(geo, diag, enc_wide, mixing_weight, gain, zonal.reshape(chunks(FLAT)))
     synth = synth.reshape(BANDS * KM, WIDE)
-    predicted, slope = grid_stage(own_live, synth, c, x, enct, dect)
-
-    everyone = exchange(predicted, "member").reshape(MEMBERS, 2, FIELDS, NLON)
     padded = jnp.pad(observed, ((0, 0), (0, 1), (0, 0)))
     truth = jnp.transpose(lax.dynamic_slice_in_dim(padded, member * 2, 2, 1), (1, 0, 2))
-    area = lax.dynamic_slice_in_dim(own_area, member * 2, 2)
-    share = score_stage(area, everyone, truth)
-    score = exchange(share.reshape(16, FIELDS, NLON), "member")
-
-    grads = grad_stage(score, slope, c, dec).reshape(chunks(WIDE))
-    grads = backward(enct_wide, mixing_weight.T, gain, leg, legt, grads)
+    prediction, score, grads = middle(own_live, own_area, synth, c, x, truth, enct, dect, dec)
+
+    grads = backward(
+        enct_wide, mixing_weight.T, gain, leg, legt, grads.reshape(chunks(WIDE))
+    )
     grads = grads.reshape(BANDS * KM, FLAT)
     result = final_stage(own_weight, own_live, grads, c, score, dec, enc)
-    prediction = jnp.transpose(predicted[:BAND], (1, 0, 2))[None]
-    return (prediction, jnp.transpose(result, (1, 0, 2))[None])
+    return (prediction[None], jnp.transpose(result, (1, 0, 2))[None])
 
 
 def solution(mesh):

time: 347 us -> 317 us (0.914)
  waiting for transfers between devices: 37.4 us -> 0 us
  Pallas kernels: 261 us -> 291 us
  starting transfers between devices: 10.4 us -> 0 us
  local copies, waits for them, and re-layouts: 25.2 us -> 15.8 us
    all_to_all x2 -> x0, waiting for transfers between devices: 37.4 us -> none  [exchange(): return lax.all_to_all(array, axis, split_axis=0, concat_axis=0, tiled=True)]
    pallas_call x3 -> x1, Pallas kernels: 28.6 us -> 57.7 us  [middle(): pl.pallas_call(middle_kernel, in_specs=[SMEM] * 2 + [VMEM] * 7, out_specs...]
    all_to_all x2 -> x0, starting transfers between devices: 10.4 us -> none  [exchange(): return lax.all_to_all(array, axis, split_axis=0, concat_axis=0, tiled=True)]
    unnamed x28 -> x32, local copies, waits for them, and re-layouts: 15.3 us -> 9.01 us
  transfers between devices with their start and end apart: 2 -> 0, of which waited for: 2 -> 0; matrix products, arithmetic and copies ran while one was open for 4% -> 0% of each run, Pallas kernels for 0% -> 0%
where the time goes in v3:
time: 317 us; the launch traced here: 316 us
  Pallas kernels  291 us (92%)
  local copies, waits for them, and re-layouts  15.8 us (5%)
  other arithmetic  4.51 us (1%)
  matrix products  4.43 us (1%)
    pallas_call x1, Pallas kernels, forward(): pl.pallas_call(forward_kernel, in_specs=[VMEM] * 6, out_specs=[ANY] * 3,...  114 us
    pallas_call x1, Pallas kernels, backward(): pl.pallas_call(backward_kernel, in_specs=[VMEM] * 3 + [ANY] * 2 + [VMEM],...  111 us
    pallas_call x1, Pallas kernels, middle(): pl.pallas_call(middle_kernel, in_specs=[SMEM] * 2 + [VMEM] * 7, out_specs...  57.7 us
    unnamed x32, local copies, waits for them, and re-layouts  9.01 us
    pallas_call x1, Pallas kernels, final_stage(): pl.pallas_call(final_kernel, in_specs=[SMEM, SMEM] + [pl.BlockSpec(memory...  8.17 us

profile of v3, /device:TPU:7, one launch (start us, length us, event | category | flops | bytes accessed | tf_op | source)
XLA Modules:
  0.0 316.4 jit_solution(2669448472631182704)
XLA Ops:
  0.6 0.8 dynamic_slice.6
  1.4 0.7 broadcast_in_dim.58.diag_ref
  2.1 1.3 fusion.10
  3.4 1.8 select_multiply_fusion
  5.2 0.0 copy-start.10
  5.2 0.1 select_reduce_fusion
  5.3 2.0 copy.40
  7.3 0.0 copy-done.10
  7.3 0.0 copy-start
  7.3 0.0 copy-start.1
  7.4 2.0 reshape.134
  9.4 0.1 copy-done.1
  9.5 0.0 copy-start.11
  9.5 0.0 copy-start.9
  9.5 0.0 copy-start.6
  9.5 4.4 %fusion = bf16[1152,768]{0,1:T(8,128)(2,1)} fusion(bf16[768,720]{1,0:T(8,128)(2,1)S(1)} %copy-done.1, f32[1152]{0:T(1024)S(1)} %select_reduce_fusion, bf16[1095,720]{1,0:T(8,128)(2,1)} %reshape.134), kind=kOutput, calls=%fused_computation.1 | convolution fusion | flops 1275789312 | bytes 4456800 | tf_op jit(solution)/shard_map/aj,bj->ab/dot_general | solution.py:567
  13.9 0.0 copy-done
  13.9 0.0 copy-start.2
  13.9 0.0 copy-done.11
  14.0 0.1 select_reduce_fusion.1
  14.0 0.1 maximum_log_fusion
  14.2 0.6 stack.10.geo_ref
  14.8 0.0 copy-done.9
  14.8 0.1 copy.29
  14.9 0.0 copy-start.4
  14.9 0.1 copy.39
  15.0 0.6 pad.16.clone.enc_ref
  15.7 0.0 copy-done.6
  15.7 0.7 pad.17.gain_ref
  16.4 113.7 %forward.1 = (bf16[3,32,8,1920]{3,2,1,0:T(8,128)(2,1)}, bf16[12,384,512]{2,1,0:T(8,128)(2,1)}, bf16[12,512,384]{2,1,0:T(8,128)(2,1)}) custom-call(f32[8,512]{1,0:T(8,128)} %stack.10.geo_ref, f32[16,128]{1,0:T(8,128)} %broadcast_in_dim.58.diag_ref, bf16[128,128]{1,0:T(8,128)(2,1)} %pad.16.clone.enc_ref, bf16[128,128]{1,0:T(8,128)(2,1)} %mix_ref.1, ...), custom_call_target="tpu_custom_call" | custom-call | tf_op jit(solution)/shard_map/forward/pallas_call | solution.py:328
  130.1 0.0 copy-done.2
  130.1 0.5 copy.32
  130.7 0.0 copy-done.4
  130.7 0.0 copy-start.8
  130.7 0.7 fusion.2.o_ref
  131.4 1.1 fusion.11.live_ref
  132.5 0.0 copy-done.8
  132.5 0.7 copy.34.dec_ref
  133.2 0.0 copy-start.5
  133.2 0.0 copy-start.7
  133.2 57.7 %middle.1 = (bf16[73,15,720]{2,1,0:T(8,128)(2,1)}, bf16[2,8,73,720]{3,2,1,0:T(8,128)(2,1)}, bf16[768,1920]{1,0:T(8,128)(2,1)}) custom-call(f32[16]{0:T(128)} %fusion.11.live_ref, f32[16]{0:T(128)} %get-tuple-element.27.area_ref, bf16[768,1920]{1,0:T(8,128)(2,1)} %bitcast.30, bf16[768,720]{1,0:T(8,128)(2,1)} %constant.86.clone.c_ref, ...), custom_call_target="tpu_custom_call" | custom-call | tf_op jit(solution)/shard_map/middle/pallas_call | solution.py:481
  190.9 0.0 copy-done.5
  190.9 0.6 pad_bitcast_fusion.enct_ref
  191.5 0.0 copy-done.7
  191.5 0.7 copy.35
  192.2 111.4 %backward.1 = bf16[3,32,8,1152]{3,2,1,0:T(8,128)(2,1)} custom-call(bf16[128,128]{1,0:T(8,128)(2,1)} %pad_bitcast_fusion.enct_ref, bf16[128,128]{1,0:T(8,128)(2,1)} %bitcast.34, f32[384,128]{1,0:T(8,128)} %pad.17.gain_ref, bf16[12,384,512]{2,1,0:T(8,128)(2,1)} %get-tuple-element.10.leg_in, bf16[12,512,384]{2,1,0:T(8,128)(2,1)} %get-tuple-element.11.legt_in, ...), custom_call_target="tpu_custom_call" | custom-call | tf_op jit(solution)/shard_map/backward/pallas_call | solution.py:341
  303.6 8.2 %final_stage.1 = bf16[15,73,720]{2,1,0:T(8,128)(2,1)} custom-call(f32[16]{0:T(128)} %copy-done.10, f32[16]{0:T(128)} %fusion.11.live_ref, bf16[768,1152]{1,0:T(8,128)(2,1)} %bitcast.28, bf16[768,720]{1,0:T(8,128)(2,1)} %constant.86.clone.c_ref, bf16[2,8,73,720]{3,2,1,0:T(8,128)(2,1)} %get-tuple-element.13.g_ref, bf16[128,73]{1,0:T(8,128)(2,1)} %copy.34.dec_ref, ...), custom_call_target="tpu_custom_call" | custom-call | tf_op jit(solution)/shard_map/final_stage/pallas_call | solution.py:514
  311.8 0.0 copy-start.3
  311.8 3.4 %copy.37 = bf16[1,73,15,720]{3,2,1,0:T(8,128)(2,1)} copy(bf16[1,73,15,720]{3,1,2,0:T(8,128)(2,1)} %bitcast.27) | data formatting | bytes 3153600
  315.2 0.0 copy-done.3
  315.2 1.2 copy.42
  (5 shorter events, 0.0 us)
Async XLA Ops:
  5.2 2.1 copy-start.10
  7.3 6.6 %copy-start = (bf16[1,73,15,720]{3,1,2,0:T(8,128)(2,1)}, bf16[1,73,15,720]{3,1,2,0:T(8,128)(2,1)S(1)}, u32[]{:S(2)}) copy-start(bf16[1,73,15,720]{3,1,2,0:T(8,128)(2,1)S(1)} %copy.40) | copy-start | bytes 4730404
  7.3 2.2 copy-start.1
  9.5 4.4 %copy-start.11 = (s32[32]{0:T(128)S(1)}, s32[32]{0:T(128)}, u32[]{:S(2)}) copy-start(s32[32]{0:T(128)} %param.11) | copy-start | bytes 388
  9.5 5.3 %copy-start.9 = (bf16[73,128]{1,0:T(8,128)(2,1)S(1)}, bf16[73,128]{1,0:T(8,128)(2,1)}, u32[]{:S(2)}) copy-start(bf16[73,128]{1,0:T(8,128)(2,1)} %enc_ref.1) | copy-start | bytes 56068
  9.5 6.2 %copy-start.6 = (f32[368,128]{1,0:T(8,128)S(1)}, f32[368,128]{1,0:T(8,128)}, u32[]{:S(2)}) copy-start(f32[368,128]{1,0:T(8,128)} %param.14) | copy-start | bytes 565252
  13.9 116.2 %copy-start.2 = (bf16[73,15,720]{2,1,0:T(8,128)(2,1)S(1)}, bf16[73,15,720]{2,1,0:T(8,128)(2,1)}, u32[]{:S(2)}) copy-start(bf16[73,15,720]{2,1,0:T(8,128)(2,1)} %param.10) | copy-start | bytes 4730404
  14.9 115.7 %copy-start.4 = (bf16[73,128]{0,1:T(8,128)(2,1)}, bf16[73,128]{0,1:T(8,128)(2,1)S(1)}, u32[]{:S(2)}) copy-start(bf16[73,128]{0,1:T(8,128)(2,1)S(1)} %copy.29) | copy-start | bytes 56068
  130.7 1.8 copy-start.8
  133.2 57.7 %copy-start.5 = (bf16[73,128]{0,1:T(8,128)(2,1)S(1)}, bf16[73,128]{0,1:T(8,128)(2,1)}, u32[]{:S(2)}) copy-start(bf16[73,128]{0,1:T(8,128)(2,1)} %copy-done.4) | copy-start | bytes 56068
  133.2 58.3 %copy-start.7 = (bf16[128,128]{1,0:T(8,128)(2,1)S(1)}, bf16[128,128]{1,0:T(8,128)(2,1)}, u32[]{:S(2)}) copy-start(bf16[128,128]{1,0:T(8,128)(2,1)} %mix_ref.1) | copy-start | bytes 98308
  311.8 3.4 %copy-start.3 = (bf16[73,15,720]{2,1,0:T(8,128)(2,1)S(1)}, bf16[73,15,720]{2,1,0:T(8,128)(2,1)}, u32[]{:S(2)}) copy-start(bf16[73,15,720]{2,1,0:T(8,128)(2,1)} %get-tuple-element.9) | copy-start | bytes 4730404

commit v4 on v3

--- a/solution.py
+++ b/solution.py
@@ -24,6 +24,8 @@
 GM = MDEV // GROUPS
 GK = 2 * GM
 MESH = pl.DeviceIdType.MESH
+IDLE = (3, 9, 16, 22, 29)
+BUSY = BANDS - len(IDLE)
 FLAT = 1152
 WIDE = BAND * CH
 
@@ -37,31 +39,71 @@
 
 
 SMEM = pl.BlockSpec(memory_space=pltpu.SMEM)
+VMEM = pl.BlockSpec(memory_space=pltpu.VMEM)
+ANY = pl.BlockSpec(memory_space=pl.ANY)
+TILES = [(t * 128, min(128, NLON - t * 128)) for t in range(6)]
+
+
+def group_orders():
+    first = np.zeros((GROUPS, BANDS), np.int64)
+    first[:2] = np.arange(2 * BANDS).reshape(2, BANDS) * GM
+    rank = 2 * BANDS
+    for owner in range(BANDS):
+        idle = owner in IDLE
+        first[2, owner] = (GROUPS * BANDS - 1 if idle else rank) * GM
+        rank += 0 if idle else 1
+    return first
+
+
+def is_idle(device):
+    found = device == IDLE[0]
+    for other in IDLE[1:]:
+        found = jnp.logical_or(found, device == other)
+    return found
+
+
+def first_of_group(group, device):
+    skipped = sum(jnp.where(device > other, 1, 0) for other in IDLE)
+    last = jnp.where(is_idle(device), GROUPS * BANDS - 1, 2 * BANDS + device - skipped)
+    return jnp.where(group == 2, last, group * BANDS + device) * GM
 
 
 def fourier_table():
-    orders = np.arange(BANDS * MDEV)
-    angle = 2.0 * np.pi * ((orders[:, None] * np.arange(NLON)[None, :]) % NLON) / NLON
-    live = (orders <= LMAX)[:, None]
+    orders = group_orders()[:, :, None] + np.arange(GM)
+    angle = 2.0 * np.pi * ((orders[..., None] * np.arange(NLON)) % NLON) / NLON
+    live = (orders <= LMAX)[..., None]
     both = np.stack([np.where(live, np.cos(angle), 0.0), np.where(live, -np.sin(angle), 0.0)])
-    both = both.reshape(2, BANDS, GROUPS, GM, NLON).transpose(2, 1, 0, 3, 4)
-    both = both.reshape(BANDS * KM, NLON)
+    both = both.transpose(1, 2, 0, 3, 4).reshape(BANDS * KM, NLON)
     return jnp.asarray(both.astype(np.float32), BF16)
 
 
 def diagonal_logs():
     k = np.arange(1, BANDS * MDEV + 16, dtype=np.float64)
     steps = 0.5 * np.log((2.0 * k + 1.0) / (2.0 * k))
-    return np.concatenate([[0.0], np.cumsum(steps)]).astype(np.float32) + np.float32(
+    logs = np.concatenate([[0.0], np.cumsum(steps)]).astype(np.float32) + np.float32(
         0.5 * math.log(0.5)
     )
-
-
-def legendre_rows(first_order, geo_ref, diag_ref, table):
+    first = group_orders()
+    orders = np.stack([first[0], first[1], first[2], first[2]])[:, :, None] + np.arange(GM)
+    orders = orders.transpose(1, 0, 2).reshape(BANDS, 16)
+    return np.broadcast_to(logs[orders][:, :, None], (BANDS, 16, 128))
+
+
+def legendre_rows(geo_ref, diag_ref, table):
+    band = lax.axis_index("space")
     cosine = jnp.broadcast_to(geo_ref[0:1, :], (16, PTS))
     log_sine = geo_ref[1:2, :]
     live = jnp.broadcast_to(geo_ref[2:3, :], (16, PTS))
-    orders = first_order + lax.broadcasted_iota(jnp.int32, (16, 128), 0)
+    sublane = lax.broadcasted_iota(jnp.int32, (16, 128), 0)
+    orders = jnp.where(
+        sublane < GM,
+        first_of_group(0, band) + sublane,
+        jnp.where(
+            sublane < 2 * GM,
+            first_of_group(1, band) + sublane - GM,
+            first_of_group(2, band) + jnp.bitwise_and(sublane, GM - 1),
+        ),
+    )
     order_f = orders.astype(F32)
     order_sq = order_f * order_f
 
@@ -130,7 +172,42 @@
     pl.semaphore_wait(barrier, BANDS - 1)
 
 
-def send_group(source, target, group, sent, got):
+def send_in(source, target, group, sent, got):
+    band, member = lax.axis_index("space"), lax.axis_index("member")
+
+    def send(i, carry):
+        peer = lax.rem(band + i, BANDS)
+
+        def start():
+            pltpu.make_async_remote_copy(
+                src_ref=source.at[group, peer],
+                dst_ref=target.at[group, band],
+                send_sem=sent.at[group],
+                recv_sem=got.at[group],
+                device_id=(member, peer),
+                device_id_type=MESH,
+            ).start()
+
+        if group == 2:
+            pl.when(jnp.logical_not(is_idle(peer)))(start)
+        else:
+            start()
+        return carry
+
+    lax.fori_loop(1, BANDS, send, 0)
+
+    def own():
+        pltpu.make_async_copy(
+            source.at[group, band], target.at[group, band], got.at[group]
+        ).start()
+
+    if group == 2:
+        pl.when(jnp.logical_not(is_idle(band)))(own)
+    else:
+        own()
+
+
+def send_out(source, target, group, sent, got):
     band, member = lax.axis_index("space"), lax.axis_index("member")
 
     def send(i, carry):
@@ -149,15 +226,40 @@
     pltpu.make_async_copy(source.at[group, band], target.at[group, band], got.at[group]).start()
 
 
-def wait_arrived(source, target, group, got):
-    pltpu.make_async_copy(source.at[group], target.at[group], got.at[group]).wait()
-
-
-def wait_sent(source, target, group, sent):
-    most = pl.ds(0, BANDS - 1)
-    pltpu.make_async_copy(
-        source.at[group, most], target.at[group, most], sent.at[group]
-    ).wait()
+def wait_chunks(array, group, count, sem):
+    part = array.at[group, pl.ds(0, count)]
+    pltpu.make_async_copy(part, part, sem.at[group]).wait()
+
+
+def wait_sent(first, second, sent_first, sent_second):
+    for group in range(2):
+        wait_chunks(first, group, BANDS - 1, sent_first)
+        wait_chunks(second, group, BANDS - 1, sent_second)
+    idle = is_idle(lax.axis_index("space"))
+
+    @pl.when(idle)
+    def _():
+        wait_chunks(first, 2, BUSY, sent_first)
+
+    @pl.when(jnp.logical_not(idle))
+    def _():
+        wait_chunks(first, 2, BUSY - 1, sent_first)
+        wait_chunks(second, 2, BANDS - 1, sent_second)
+
+
+def clear_idle(target):
+    for owner in IDLE:
+        target[2, owner] = jnp.zeros(target.shape[2:], BF16)
+
+
+def each_busy_group(work):
+    idle = is_idle(lax.axis_index("space"))
+
+    def one_group(group, carry):
+        pl.when(jnp.logical_not(jnp.logical_and(group == 2, idle)))(lambda: work(group))
+        return carry
+
+    lax.fori_loop(0, GROUPS, one_group, 0)
 
 
 def gather_points(rows, points, order):
@@ -183,11 +285,12 @@
     geo_ref, diag_ref, enc_ref, mix_ref, gain_ref, z_ref, out_ref, leg_out, legt_out,
     table, leg, legt, arrived, rows, points, made, ready, sent_in, got_in, sent_out, got_out, kept
 ):
-    first_order = lax.axis_index("space") * MDEV
+    band = lax.axis_index("space")
     enter()
     for group in range(GROUPS):
-        send_group(z_ref, arrived, group, sent_in, got_in)
-    legendre_rows(first_order, geo_ref, diag_ref, table)
+        send_in(z_ref, arrived, group, sent_in, got_in)
+    clear_idle(out_ref)
+    legendre_rows(geo_ref, diag_ref, table)
     legendre_tables(table, leg, legt)
     save = pltpu.make_async_copy(leg, leg_out, kept.at[0])
     save_t = pltpu.make_async_copy(legt, legt_out, kept.at[1])
@@ -195,8 +298,9 @@
     save_t.start()
     points[...] = jnp.zeros((PTS, 256), BF16)
 
-    def one_group(group, carry):
-        wait_arrived(z_ref, arrived, group, got_in)
+    def one_group(group):
+        wait_chunks(arrived, group, BANDS, got_in)
+        first_order = first_of_group(group, band)
         for r in range(BAND):
             base, off = window(r)
             pair = arrived[group, :, :, base : base + 256].astype(F32).reshape(BANDS * GK, 256)
@@ -206,7 +310,7 @@
             m = group * GM + order
             gather_points(rows, points, order)
             coeffs = dot(leg[m], points[...], 1, 0).astype(BF16)
-            gain = gain_ref[...] * order_factor(first_order + m)
+            gain = padded_gain(gain_ref) * order_factor(first_order + order)
             filtered = []
             for k in range(2):
                 channels = dot(coeffs[:, k * 128 : (k + 1) * 128], enc_ref[...], 1, 0).astype(BF16)
@@ -219,36 +323,47 @@
             ready[group, :, :, r * CH : (r + 1) * CH] = (
                 made[r].reshape(BANDS, GK, CH).astype(BF16)
             )
-        send_group(ready, out_ref, group, sent_out, got_out)
-        return carry
-
-    lax.fori_loop(0, GROUPS, one_group, 0)
+        send_out(ready, out_ref, group, sent_out, got_out)
+
+    each_busy_group(one_group)
     save.wait()
     save_t.wait()
+    wait_sent(z_ref, ready, sent_in, sent_out)
     for group in range(GROUPS):
-        wait_sent(z_ref, arrived, group, sent_in)
-        wait_sent(ready, out_ref, group, sent_out)
-        wait_arrived(ready, out_ref, group, got_out)
+        wait_chunks(out_ref, group, BUSY if group == 2 else BANDS, got_out)
+
+
+def padded_gain(gain_ref):
+    rows = gain_ref.shape[0]
+    return jnp.concatenate([gain_ref[...], jnp.zeros((DEG - rows, CH), F32)], axis=0)
 
 
 def backward_kernel(
-    enct_ref, mixt_ref, gain_ref, leg_in, legt_in, z_ref, out_ref,
-    leg, legt, arrived, rows, points, made, ready, sent_in, got_in, sent_out, got_out, kept
+    weight_ref, live_ref, enct_ref, mixt_ref, gain_ref, enc_ref, dec_ref, c_ref, g_ref,
+    leg_in, legt_in, z_ref, out_ref,
+    leg, legt, arrived, rows, points, made, ready, sent_in, got_in, sent_out, got_out, kept,
+    returned, spread, local, wide_rows,
 ):
-    first_order = lax.axis_index("space") * MDEV
+    band = lax.axis_index("space")
     load = pltpu.make_async_copy(leg_in, leg, kept.at[0])
     load_t = pltpu.make_async_copy(legt_in, legt, kept.at[1])
     load.start()
     load_t.start()
     enter()
     for group in range(GROUPS):
-        send_group(z_ref, arrived, group, sent_in, got_in)
+        send_in(z_ref, arrived, group, sent_in, got_in)
+    clear_idle(returned)
     points[...] = jnp.zeros((PTS, 256), BF16)
+    for r in range(BAND):
+        score = g_ref[r % 2, r // 2]
+        block = dot(dec_ref[...], score, 1, 0).astype(BF16)
+        local[r] = score.astype(F32) + dot(enc_ref[...], block, 1, 0)
     load.wait()
     load_t.wait()
 
-    def one_group(group, carry):
-        wait_arrived(z_ref, arrived, group, got_in)
+    def one_group(group):
+        wait_chunks(arrived, group, BANDS, got_in)
+        first_order = first_of_group(group, band)
         for r in range(BAND):
             rows[r] = (
                 arrived[group, :, :, r * CH : (r + 1) * CH].astype(F32).reshape(BANDS * GK, CH)
@@ -258,7 +373,7 @@
             m = group * GM + order
             gather_points(rows, points, order)
             grads = dot(leg[m], points[...], 1, 0)
-            gain = gain_ref[...] * order_factor(first_order + m)
+            gain = padded_gain(gain_ref) * order_factor(first_order + order)
             back = []
             for k in range(2):
                 scaled = (grads[:, k * 128 : (k + 1) * 128] * gain).astype(BF16)
@@ -286,18 +401,25 @@
             spill = moved[:, 128:]
         put(at, low)
         put(at + 128, spill)
-        send_group(ready, out_ref, group, sent_out, got_out)
-        return carry
-
-    lax.fori_loop(0, GROUPS, one_group, 0)
+        send_out(ready, returned, group, sent_out, got_out)
+
+    each_busy_group(one_group)
     for group in range(GROUPS):
-        wait_sent(z_ref, arrived, group, sent_in)
-        wait_sent(ready, out_ref, group, sent_out)
-        wait_arrived(ready, out_ref, group, got_out)
-
-
-VMEM = pl.BlockSpec(memory_space=pltpu.VMEM)
-ANY = pl.BlockSpec(memory_space=pl.ANY)
+        wait_chunks(returned, group, BUSY if group == 2 else BANDS, got_out)
+        block = returned[group].astype(F32).reshape(BANDS * GK, FLAT).astype(BF16)
+        part = dot(block, c_ref[group * BANDS * GK : (group + 1) * BANDS * GK, :], 0, 0)
+        spread[...] = part if group == 0 else spread[...] + part
+    for r in range(BAND):
+        far = spread[r * FIELDS : (r + 1) * FIELDS, :] * weight_ref[r]
+        result = (local[r] + far) * live_ref[r]
+        for t, (start, size) in enumerate(TILES):
+            wide_rows[t, pl.ds(r, FIELDS, stride=16), :size] = result[:, start : start + size]
+    for t, (start, size) in enumerate(TILES):
+        whole = wide_rows[t].reshape(FIELDS, 16, 128)
+        out_ref[:, :, start : start + size] = whole[:, :BAND, :size].astype(BF16)
+    wait_sent(z_ref, ready, sent_in, sent_out)
+
+
 LEG = jax.ShapeDtypeStruct((MDEV, DEG, PTS), BF16)
 LEGT = jax.ShapeDtypeStruct((MDEV, PTS, DEG), BF16)
 
@@ -328,7 +450,7 @@
     return pl.pallas_call(
         forward_kernel,
         in_specs=[VMEM] * 6,
-        out_specs=[ANY] * 3,
+        out_specs=[VMEM, ANY, ANY],
         out_shape=[jax.ShapeDtypeStruct(chunks(WIDE), BF16), LEG, LEGT],
         scratch_shapes=[pltpu.VMEM((PTS // 128, DEG * 16, 128), F32)]
         + spectral_scratch(FLAT, WIDE),
@@ -337,19 +459,22 @@
     )(geo, diag, enc, mix, gain, z)
 
 
-def backward(enct, mixt, gain, leg, legt, z):
+def backward(weight, live, enct, mixt, gain, enc, dec, c, score, leg, legt, z):
     return pl.pallas_call(
         backward_kernel,
-        in_specs=[VMEM] * 3 + [ANY] * 2 + [VMEM],
-        out_specs=ANY,
-        out_shape=jax.ShapeDtypeStruct(chunks(FLAT), BF16),
-        scratch_shapes=spectral_scratch(WIDE, FLAT),
+        in_specs=[SMEM] * 2 + [VMEM] * 7 + [ANY] * 2 + [VMEM],
+        out_specs=VMEM,
+        out_shape=jax.ShapeDtypeStruct((FIELDS, BAND, NLON), BF16),
+        scratch_shapes=spectral_scratch(WIDE, FLAT)
+        + [
+            pltpu.VMEM(chunks(FLAT), BF16),
+            pltpu.VMEM((FLAT, NLON), F32),
+            pltpu.VMEM((BAND, FIELDS, NLON), F32),
+            pltpu.VMEM((len(TILES), FIELDS * 16, 128), F32),
+        ],
         compiler_params=remote_params(2),
         name="backward",
-    )(enct, mixt, gain, leg, legt, z)
-
-
-TILES = [(t * 128, min(128, NLON - t * 128)) for t in range(6)]
+    )(weight, live, enct, mixt, gain, enc, dec, c, score, leg, legt, z)
 
 
 def score_tile(p_ref, o_ref, out_ref, group, lanes, area):
@@ -500,34 +625,11 @@
     )(live, area, s, c, x, truth, enct, dect, dec)
 
 
-def final_kernel(weight_ref, live_ref, z_ref, c_ref, g_ref, dec_ref, enc_ref, out_ref, spread):
-    spread[...] = dot(z_ref[...], c_ref[...], 0, 0)
-    for r in range(BAND):
-        score = g_ref[r % 2, r // 2]
-        block = dot(dec_ref[...], score, 1, 0).astype(BF16)
-        local = dot(enc_ref[...], block, 1, 0)
-        far = spread[r * FIELDS : (r + 1) * FIELDS, :] * weight_ref[r]
-        out_ref[r] = ((score.astype(F32) + local + far) * live_ref[r]).astype(BF16)
-
-
-def final_stage(weight, live, z, c, score, dec, enc):
-    return pl.pallas_call(
-        final_kernel,
-        in_specs=[SMEM, SMEM] + [pl.BlockSpec(memory_space=pltpu.VMEM)] * 5,
-        out_specs=pl.BlockSpec(memory_space=pltpu.VMEM),
-        out_shape=jax.ShapeDtypeStruct((BAND, FIELDS, NLON), BF16),
-        scratch_shapes=[pltpu.VMEM((FLAT, NLON), F32)],
-        compiler_params=pltpu.CompilerParams(vmem_limit_bytes=56 * 1024 * 1024),
-        name="final_stage",
-    )(weight, live, z, c, score, dec, enc)
-
-
 def on_device(
     states, observed, band_rows, encoder_weight, mixing_weight, degree_gain, decoder_weight
 ):
     band = lax.axis_index("space")
     member = lax.axis_index("member")
-    first = band * MDEV
 
     number = jnp.arange(BANDS, dtype=jnp.int32)
     point = jnp.arange(PTS, dtype=jnp.int32)
@@ -549,9 +651,7 @@
     own_area = 8.0 * own_sine * own_live
 
     c = fourier_table()
-    diag = lax.dynamic_slice_in_dim(jnp.asarray(diagonal_logs()), first, 16)
-    diag = jnp.broadcast_to(diag[:, None], (16, 128))
-    gain = jnp.pad(degree_gain, ((0, DEG - degree_gain.shape[0]), (0, 0)))
+    diag = lax.dynamic_index_in_dim(jnp.asarray(diagonal_logs()), band, 0, keepdims=False)
     enc = encoder_weight
     enct = enc.T
     dec = decoder_weight
@@ -567,18 +667,19 @@
         jnp.einsum("aj,bj->ab", c, flat, preferred_element_type=F32) * lane_weight[None]
     ).astype(BF16)
 
-    synth, leg, legt = forward(geo, diag, enc_wide, mixing_weight, gain, zonal.reshape(chunks(FLAT)))
+    synth, leg, legt = forward(
+        geo, diag, enc_wide, mixing_weight, degree_gain, zonal.reshape(chunks(FLAT))
+    )
     synth = synth.reshape(BANDS * KM, WIDE)
     padded = jnp.pad(observed, ((0, 0), (0, 1), (0, 0)))
     truth = jnp.transpose(lax.dynamic_slice_in_dim(padded, member * 2, 2, 1), (1, 0, 2))
     prediction, score, grads = middle(own_live, own_area, synth, c, x, truth, enct, dect, dec)
 
-    grads = backward(
-        enct_wide, mixing_weight.T, gain, leg, legt, grads.reshape(chunks(WIDE))
+    result = backward(
+        own_weight, own_live, enct_wide, mixing_weight.T, degree_gain, enc, dec, c, score,
+        leg, legt, grads.reshape(chunks(WIDE)),
     )
-    grads = grads.reshape(BANDS * KM, FLAT)
-    result = final_stage(own_weight, own_live, grads, c, score, dec, enc)
-    return (prediction[None], jnp.transpose(result, (1, 0, 2))[None])
+    return (prediction[None], result[None])
 
 
 def solution(mesh):

time: 317 us -> 308 us (0.972)
  Pallas kernels: 291 us -> 284 us
    pallas_call x3 -> x2, Pallas kernels: 233 us -> 227 us  [the longest x1 114 us: backward(): pl.pallas_call(backward_kernel, in_specs=[SMEM] * 2 + [VMEM] * 7 + [ANY]...]
where the time goes in v4:
time: 308 us
  Pallas kernels  284 us (92%)
  local copies, waits for them, and re-layouts  13.9 us (5%)
  other arithmetic  4.65 us (2%)
  matrix products  4.41 us (1%)
    pallas_call x1, Pallas kernels, backward(): pl.pallas_call(backward_kernel, in_specs=[SMEM] * 2 + [VMEM] * 7 + [ANY]...  114 us
    pallas_call x1, Pallas kernels, forward(): pl.pallas_call(forward_kernel, in_specs=[VMEM] * 6, out_specs=[VMEM, ANY,...  113 us
    pallas_call x1, Pallas kernels, middle(): pl.pallas_call(middle_kernel, in_specs=[SMEM] * 2 + [VMEM] * 7, out_specs...  57.4 us
    unnamed x32, local copies, waits for them, and re-layouts  7.75 us

profile of v4, /device:TPU:7, one launch (start us, length us, event | category | flops | bytes accessed | tf_op | source)
XLA Modules:
  0.0 307.8 jit_solution(5889792795177023001)
XLA Ops:
  0.6 1.3 fusion.10
  2.0 1.8 select_multiply_fusion
  3.8 0.0 copy-start.10
  3.8 0.1 select_reduce_fusion
  3.9 2.0 copy.37
  6.0 0.0 copy-done.10
  6.0 0.0 copy-start
  6.0 0.0 copy-start.2
  6.0 2.0 reshape.130
  8.0 0.1 copy-done.2
  8.1 0.0 copy-start.11
  8.1 0.0 copy-start.8
  8.1 4.4 %fusion = bf16[1152,768]{0,1:T(8,128)(2,1)} fusion(bf16[768,720]{1,0:T(8,128)(2,1)S(1)} %copy-done.2, f32[1152]{0:T(1024)S(1)} %select_reduce_fusion, bf16[1095,720]{1,0:T(8,128)(2,1)} %reshape.130), kind=kOutput, calls=%fused_computation.1 | convolution fusion | flops 1275789312 | bytes 4456800 | tf_op jit(solution)/shard_map/aj,bj->ab/dot_general | solution.py:667
  12.5 0.0 copy-done
  12.5 0.0 copy-start.3
  12.5 0.8 dynamic-slice_bitcast_fusion
  13.4 0.7 broadcast.219.diag_ref
  14.0 0.0 copy-done.11
  14.0 0.1 select_reduce_fusion.1
  14.1 0.1 maximum_log_fusion
  14.3 0.6 stack.10.geo_ref
  14.9 0.0 copy-done.8
  14.9 0.1 copy.27
  15.0 0.0 copy-start.5
  15.0 0.1 copy.36
  15.1 0.6 pad.12.clone.enc_ref
  15.8 112.6 %forward.1 = (bf16[3,32,8,1920]{3,2,1,0:T(8,128)(2,1)}, bf16[12,384,512]{2,1,0:T(8,128)(2,1)}, bf16[12,512,384]{2,1,0:T(8,128)(2,1)}) custom-call(f32[8,512]{1,0:T(8,128)} %stack.10.geo_ref, f32[16,128]{1,0:T(8,128)} %broadcast.219.diag_ref, bf16[128,128]{1,0:T(8,128)(2,1)} %pad.12.clone.enc_ref, bf16[128,128]{1,0:T(8,128)(2,1)} %mix_ref.1, ...), custom_call_target="tpu_custom_call" | custom-call | tf_op jit(solution)/shard_map/forward/pallas_call | solution.py:450
  128.4 0.0 copy-done.3
  128.4 0.5 copy.30
  128.9 0.0 copy-done.5
  128.9 0.0 copy-start.9
  129.0 0.7 fusion.2.o_ref
  129.7 1.2 fusion.11.live_ref
  130.9 0.0 copy-done.9
  130.9 0.7 copy.32.dec_ref
  131.6 0.0 copy-start.6
  131.6 0.0 copy-start.7
  131.6 57.4 %middle.1 = (bf16[73,15,720]{2,1,0:T(8,128)(2,1)}, bf16[2,8,73,720]{3,2,1,0:T(8,128)(2,1)}, bf16[768,1920]{1,0:T(8,128)(2,1)}) custom-call(f32[16]{0:T(128)} %fusion.11.live_ref, f32[16]{0:T(128)} %get-tuple-element.21.area_ref, bf16[768,1920]{1,0:T(8,128)(2,1)} %bitcast.28, bf16[768,720]{1,0:T(8,128)(2,1)} %constant.85.clone.c_ref, ...), custom_call_target="tpu_custom_call" | custom-call | tf_op jit(solution)/shard_map/middle/pallas_call | solution.py:606
  189.0 0.0 copy-done.6
  189.0 0.6 pad_bitcast_fusion.enct_ref
  189.6 0.0 copy-done.7
  189.6 0.7 copy.33
  190.3 0.0 copy-start.4
  190.3 114.1 %backward.1 = bf16[73,15,720]{2,1,0:T(8,128)(2,1)} custom-call(f32[16]{0:T(128)} %copy-done.10, f32[16]{0:T(128)} %fusion.11.live_ref, bf16[128,128]{1,0:T(8,128)(2,1)} %pad_bitcast_fusion.enct_ref, bf16[128,128]{1,0:T(8,128)(2,1)} %bitcast.32, f32[368,128]{1,0:T(8,128)} %gain_ref.3, bf16[73,128]{1,0:T(8,128)(2,1)} %enc_ref.1, ...), custom_call_target="tpu_custom_call" | custom-call | tf_op jit(solution)/shard_map/backward/pallas_call | solution.py:463
  304.4 0.0 copy-done.4
  304.4 0.0 copy-start.1
  304.4 1.2 copy.40
  305.6 0.9 copy-done.1
  306.5 1.2 copy.41
  (5 shorter events, 0.0 us)
Async XLA Ops:
  3.8 2.1 copy-start.10
  6.0 6.6 %copy-start = (bf16[1,73,15,720]{3,1,2,0:T(8,128)(2,1)}, bf16[1,73,15,720]{3,1,2,0:T(8,128)(2,1)S(1)}, u32[]{:S(2)}) copy-start(bf16[1,73,15,720]{3,1,2,0:T(8,128)(2,1)S(1)} %copy.37) | copy-start | bytes 4730404
  6.0 2.2 copy-start.2
  8.1 5.9 %copy-start.11 = (s32[32]{0:T(128)S(1)}, s32[32]{0:T(128)}, u32[]{:S(2)}) copy-start(s32[32]{0:T(128)} %param.11) | copy-start | bytes 388
  8.1 6.8 %copy-start.8 = (bf16[73,128]{1,0:T(8,128)(2,1)S(1)}, bf16[73,128]{1,0:T(8,128)(2,1)}, u32[]{:S(2)}) copy-start(bf16[73,128]{1,0:T(8,128)(2,1)} %enc_ref.1) | copy-start | bytes 56068
  12.5 115.8 %copy-start.3 = (bf16[73,15,720]{2,1,0:T(8,128)(2,1)S(1)}, bf16[73,15,720]{2,1,0:T(8,128)(2,1)}, u32[]{:S(2)}) copy-start(bf16[73,15,720]{2,1,0:T(8,128)(2,1)} %param.10) | copy-start | bytes 4730404
  15.0 113.9 %copy-start.5 = (bf16[73,128]{0,1:T(8,128)(2,1)}, bf16[73,128]{0,1:T(8,128)(2,1)S(1)}, u32[]{:S(2)}) copy-start(bf16[73,128]{0,1:T(8,128)(2,1)S(1)} %copy.27) | copy-start | bytes 56068
  128.9 1.9 copy-start.9
  131.6 57.4 %copy-start.6 = (bf16[73,128]{0,1:T(8,128)(2,1)S(1)}, bf16[73,128]{0,1:T(8,128)(2,1)}, u32[]{:S(2)}) copy-start(bf16[73,128]{0,1:T(8,128)(2,1)} %copy-done.5) | copy-start | bytes 56068
  131.6 58.0 %copy-start.7 = (bf16[128,128]{1,0:T(8,128)(2,1)S(1)}, bf16[128,128]{1,0:T(8,128)(2,1)}, u32[]{:S(2)}) copy-start(bf16[128,128]{1,0:T(8,128)(2,1)} %mix_ref.1) | copy-start | bytes 98308
  190.3 114.1 %copy-start.4 = (bf16[73,15,720]{2,1,0:T(8,128)(2,1)S(1)}, bf16[73,15,720]{2,1,0:T(8,128)(2,1)}, u32[]{:S(2)}) copy-start(bf16[73,15,720]{2,1,0:T(8,128)(2,1)} %get-tuple-element.9) | copy-start | bytes 4730404
  304.4 2.1 copy-start.1

commit v5 on v4

--- a/solution.py
+++ b/solution.py
@@ -159,7 +159,24 @@
     return start // 128 * 128, start % 128
 
 
-def enter():
+def pack_windows(rows, value_of, put):
+    low = spill = jnp.zeros((rows, 128), F32)
+    at = 0
+    for r in range(BAND):
+        base, off = window(r)
+        while at < base:
+            put(at, low)
+            low = spill
+            at += 128
+        value = value_of(r)
+        moved = pltpu.roll(jnp.concatenate([value, jnp.zeros_like(value)], axis=1), off, 1)
+        low = low + moved[:, :128]
+        spill = moved[:, 128:]
+    put(at, low)
+    put(at + 128, spill)
+
+
+def announce():
     band, member = lax.axis_index("space"), lax.axis_index("member")
     barrier = pltpu.get_barrier_semaphore()
 
@@ -169,7 +186,10 @@
         return carry
 
     lax.fori_loop(1, BANDS, signal, 0)
-    pl.semaphore_wait(barrier, BANDS - 1)
+
+
+def enter():
+    pl.semaphore_wait(pltpu.get_barrier_semaphore(), BANDS - 1)
 
 
 def send_in(source, target, group, sent, got):
@@ -282,12 +302,26 @@
 
 
 def forward_kernel(
-    geo_ref, diag_ref, enc_ref, mix_ref, gain_ref, z_ref, out_ref, leg_out, legt_out,
+    weight_ref, geo_ref, diag_ref, enc_ref, mix_ref, gain_ref, c_ref, x_ref,
+    out_ref, leg_out, legt_out, z_ref, padded,
     table, leg, legt, arrived, rows, points, made, ready, sent_in, got_in, sent_out, got_out, kept
 ):
     band = lax.axis_index("space")
-    enter()
+    announce()
+    padded[...] = jnp.zeros(padded.shape, F32)
     for group in range(GROUPS):
+        waves = c_ref[group * BANDS * GK : (group + 1) * BANDS * GK, :]
+
+        def zonal(r):
+            padded[:, :FIELDS] = dot(waves, x_ref[r], 1, 1) * weight_ref[r]
+            return padded[...]
+
+        def put_zonal(at, value):
+            z_ref[group, :, :, at : at + 128] = value.reshape(BANDS, GK, 128).astype(BF16)
+
+        pack_windows(BANDS * GK, zonal, put_zonal)
+        if group == 0:
+            enter()
         send_in(z_ref, arrived, group, sent_in, got_in)
     clear_idle(out_ref)
     legendre_rows(geo_ref, diag_ref, table)
@@ -342,13 +376,14 @@
     weight_ref, live_ref, enct_ref, mixt_ref, gain_ref, enc_ref, dec_ref, c_ref, g_ref,
     leg_in, legt_in, z_ref, out_ref,
     leg, legt, arrived, rows, points, made, ready, sent_in, got_in, sent_out, got_out, kept,
-    returned, spread, local, wide_rows,
+    returned, spread, local, wide_rows, final, stored,
 ):
     band = lax.axis_index("space")
     load = pltpu.make_async_copy(leg_in, leg, kept.at[0])
     load_t = pltpu.make_async_copy(legt_in, legt, kept.at[1])
     load.start()
     load_t.start()
+    announce()
     enter()
     for group in range(GROUPS):
         send_in(z_ref, arrived, group, sent_in, got_in)
@@ -387,20 +422,7 @@
         def put(at, value):
             ready[group, :, :, at : at + 128] = value.reshape(BANDS, GK, 128).astype(BF16)
 
-        low = spill = jnp.zeros((BANDS * GK, 128), F32)
-        at = 0
-        for r in range(BAND):
-            base, off = window(r)
-            while at < base:
-                put(at, low)
-                low = spill
-                at += 128
-            value = made[r]
-            moved = pltpu.roll(jnp.concatenate([value, jnp.zeros_like(value)], axis=1), off, 1)
-            low = low + moved[:, :128]
-            spill = moved[:, 128:]
-        put(at, low)
-        put(at + 128, spill)
+        pack_windows(BANDS * GK, lambda r: made[r], put)
         send_out(ready, returned, group, sent_out, got_out)
 
     each_busy_group(one_group)
@@ -414,10 +436,21 @@
         result = (local[r] + far) * live_ref[r]
         for t, (start, size) in enumerate(TILES):
             wide_rows[t, pl.ds(r, FIELDS, stride=16), :size] = result[:, start : start + size]
-    for t, (start, size) in enumerate(TILES):
-        whole = wide_rows[t].reshape(FIELDS, 16, 128)
-        out_ref[:, :, start : start + size] = whole[:, :BAND, :size].astype(BF16)
+    copies = []
+    for part, (low, high) in enumerate(((0, 40), (40, FIELDS))):
+        for t, (start, size) in enumerate(TILES):
+            held = wide_rows[t, low * 16 : high * 16, :].reshape(high - low, 16, 128)
+            final[low:high, :, start : start + size] = held[:, :BAND, :size].astype(BF16)
+        copies.append(
+            pltpu.make_async_copy(
+                final.at[pl.ds(low, high - low)], out_ref.at[0, pl.ds(low, high - low)],
+                stored.at[part],
+            )
+        )
+        copies[-1].start()
     wait_sent(z_ref, ready, sent_in, sent_out)
+    for copy in copies:
+        copy.wait()
 
 
 LEG = jax.ShapeDtypeStruct((MDEV, DEG, PTS), BF16)
@@ -446,31 +479,37 @@
     )
 
 
-def forward(geo, diag, enc, mix, gain, z):
+def forward(weight, geo, diag, enc, mix, gain, c, x):
     return pl.pallas_call(
         forward_kernel,
-        in_specs=[VMEM] * 6,
+        in_specs=[SMEM] + [VMEM] * 7,
         out_specs=[VMEM, ANY, ANY],
         out_shape=[jax.ShapeDtypeStruct(chunks(WIDE), BF16), LEG, LEGT],
-        scratch_shapes=[pltpu.VMEM((PTS // 128, DEG * 16, 128), F32)]
+        scratch_shapes=[
+            pltpu.VMEM(chunks(FLAT), BF16),
+            pltpu.VMEM((BANDS * GK, 128), F32),
+            pltpu.VMEM((PTS // 128, DEG * 16, 128), F32),
+        ]
         + spectral_scratch(FLAT, WIDE),
         compiler_params=remote_params(1),
         name="forward",
-    )(geo, diag, enc, mix, gain, z)
+    )(weight, geo, diag, enc, mix, gain, c, x)
 
 
 def backward(weight, live, enct, mixt, gain, enc, dec, c, score, leg, legt, z):
     return pl.pallas_call(
         backward_kernel,
         in_specs=[SMEM] * 2 + [VMEM] * 7 + [ANY] * 2 + [VMEM],
-        out_specs=VMEM,
-        out_shape=jax.ShapeDtypeStruct((FIELDS, BAND, NLON), BF16),
+        out_specs=ANY,
+        out_shape=jax.ShapeDtypeStruct((1, FIELDS, BAND, NLON), BF16),
         scratch_shapes=spectral_scratch(WIDE, FLAT)
         + [
             pltpu.VMEM(chunks(FLAT), BF16),
             pltpu.VMEM((FLAT, NLON), F32),
             pltpu.VMEM((BAND, FIELDS, NLON), F32),
             pltpu.VMEM((len(TILES), FIELDS * 16, 128), F32),
+            pltpu.VMEM((FIELDS, BAND, NLON), BF16),
+            pltpu.SemaphoreType.DMA((2,)),
         ],
         compiler_params=remote_params(2),
         name="backward",
@@ -500,7 +539,7 @@
 def middle_kernel(
     live_ref, area_ref, s_ref, c_ref, x_ref, o_ref, enct_ref, dect_ref, dec_ref,
     pred_ref, score_ref, out_ref,
-    mine, everyone, share, slope, wide_rows, sent_in, got_in, sent_out, got_out,
+    mine, everyone, share, slope, wide_rows, final, stored, sent_in, got_in, sent_out, got_out,
 ):
     band, member = lax.axis_index("space"), lax.axis_index("member")
     barrier = pltpu.get_barrier_semaphore()
@@ -555,8 +594,10 @@
         keep(mine, everyone, group, got_in)
 
     for t, (start, size) in enumerate(TILES):
-        rows = wide_rows[t].reshape(FIELDS, 16, 128)
-        pred_ref[:, :, start : start + size] = rows[:, :BAND, :size].astype(BF16)
+        held = wide_rows[t].reshape(FIELDS, 16, 128)
+        final[:, :, start : start + size] = held[:, :BAND, :size].astype(BF16)
+    store = pltpu.make_async_copy(final, pred_ref.at[0], stored.at[0])
+    store.start()
 
     def score_group(group, carry):
         pltpu.make_async_copy(mine.at[group], everyone.at[group], got_in.at[group]).wait()
@@ -593,6 +634,7 @@
                 if row < BAND:
                     out_ref[:, row * CH : (row + 1) * CH] = made[:, part * CH : (part + 1) * CH]
 
+    store.wait()
     most = pl.ds(0, MEMBERS - 1)
     for group in range(2):
         for source, target, sent in ((mine, everyone, sent_in), (share, score_ref, sent_out)):
@@ -606,9 +648,9 @@
     return pl.pallas_call(
         middle_kernel,
         in_specs=[SMEM] * 2 + [VMEM] * 7,
-        out_specs=[VMEM] * 3,
+        out_specs=[ANY, VMEM, VMEM],
         out_shape=[
-            jax.ShapeDtypeStruct((FIELDS, BAND, NLON), BF16),
+            jax.ShapeDtypeStruct((1, FIELDS, BAND, NLON), BF16),
             jax.ShapeDtypeStruct(quarter, BF16),
             jax.ShapeDtypeStruct((BANDS * KM, WIDE), BF16),
         ],
@@ -618,6 +660,8 @@
             pltpu.VMEM(quarter, BF16),
             pltpu.VMEM((2, MEMBERS, CH, NLON), BF16),
             pltpu.VMEM((len(TILES), FIELDS * 16, 128), F32),
+            pltpu.VMEM((FIELDS, BAND, NLON), BF16),
+            pltpu.SemaphoreType.DMA((1,)),
         ]
         + [pltpu.SemaphoreType.DMA((2,))] * 4,
         compiler_params=remote_params(3),
@@ -660,15 +704,8 @@
     enct_wide = enc_wide.T
 
     x = jnp.transpose(states[0], (1, 0, 2))
-    flat = jnp.pad(x.reshape(BAND * FIELDS, NLON), ((0, FLAT - BAND * FIELDS), (0, 0)))
-    lane_row = jnp.arange(FLAT, dtype=jnp.int32) // FIELDS
-    lane_weight = jnp.sum(jnp.where(row[:, None] == lane_row[None], own_weight[:, None], 0.0), axis=0)
-    zonal = (
-        jnp.einsum("aj,bj->ab", c, flat, preferred_element_type=F32) * lane_weight[None]
-    ).astype(BF16)
-
     synth, leg, legt = forward(
-        geo, diag, enc_wide, mixing_weight, degree_gain, zonal.reshape(chunks(FLAT))
+        own_weight, geo, diag, enc_wide, mixing_weight, degree_gain, c, x
     )
     synth = synth.reshape(BANDS * KM, WIDE)
     padded = jnp.pad(observed, ((0, 0), (0, 1), (0, 0)))
@@ -679,7 +716,7 @@
         own_weight, own_live, enct_wide, mixing_weight.T, degree_gain, enc, dec, c, score,
         leg, legt, grads.reshape(chunks(WIDE)),
     )
-    return (prediction[None], result[None])
+    return (prediction, result)
 
 
 def solution(mesh):

time: 308 us -> 304 us (0.987)
  matrix products: 4.41 us -> 0 us
    dot_general x1 -> x0, matrix products: 4.41 us -> none  [on_device(): jnp.einsum('aj,bj->ab', c, flat, preferred_element_type=F32)]
    unnamed x32 -> x22, local copies, waits for them, and re-layouts: 7.75 us -> 9.61 us
where the time goes in v5:
time: 304 us
  Pallas kernels  284 us (93%)
  local copies, waits for them, and re-layouts  13.6 us (4%)
  other arithmetic  5.37 us (2%)
    pallas_call x1, Pallas kernels, backward(): pl.pallas_call(backward_kernel, in_specs=[SMEM] * 2 + [VMEM] * 7 + [ANY]...  114 us
    pallas_call x1, Pallas kernels, forward(): pl.pallas_call(forward_kernel, in_specs=[SMEM] + [VMEM] * 7, out_specs=[V...  113 us
    pallas_call x1, Pallas kernels, middle(): pl.pallas_call(middle_kernel, in_specs=[SMEM] * 2 + [VMEM] * 7, out_specs...  57 us
    unnamed x22, local copies, waits for them, and re-layouts  9.61 us

profile of v5, /device:TPU:7, one launch (start us, length us, event | category | flops | bytes accessed | tf_op | source)
XLA Modules:
  0.0 303.9 jit_solution(3600730843872619739)
XLA Ops:
  0.6 1.4 fusion.5
  2.0 2.0 select_multiply_fusion
  4.0 0.7 dynamic-slice_bitcast_fusion
  4.7 0.7 broadcast.170.diag_ref
  5.3 0.7 select_reduce_fusion
  6.1 0.1 maximum_log_fusion
  6.2 0.6 stack.10.geo_ref
  6.8 0.8 copy.19
  7.7 0.0 copy-start.3
  7.7 0.1 copy.28
  7.8 0.6 pad.8.clone.enc_ref
  8.4 3.3 %copy.29 = bf16[1,73,15,720]{3,1,2,0:T(8,128)(2,1)} copy(bf16[1,73,15,720]{3,2,1,0:T(8,128)(2,1)} %param.9) | data formatting | bytes 3153600 | tf_op args[0]
  11.7 0.0 copy-done.3
  11.7 0.0 copy-start.1
  11.7 113.2 %forward.1 = (bf16[3,32,8,1920]{3,2,1,0:T(8,128)(2,1)}, bf16[12,384,512]{2,1,0:T(8,128)(2,1)}, bf16[12,512,384]{2,1,0:T(8,128)(2,1)}) custom-call(f32[16]{0:T(128)} %get-tuple-element.20.weight_ref, f32[8,512]{1,0:T(8,128)} %stack.10.geo_ref, f32[16,128]{1,0:T(8,128)} %broadcast.170.diag_ref, bf16[128,128]{1,0:T(8,128)(2,1)} %pad.8.clone.enc_ref, ...), custom_call_target="tpu_custom_call" | custom-call | tf_op jit(solution)/shard_map/forward/pallas_call | solution.py:483
  124.9 0.0 copy-done.1
  125.0 0.5 copy.22
  125.5 0.0 copy-start.6
  125.5 0.7 fusion.o_ref
  126.3 1.2 fusion.6.live_ref
  127.4 0.0 copy-done.6
  127.4 0.8 copy.24.dec_ref
  128.2 0.0 copy-start.4
  128.2 0.0 copy-start.5
  128.2 57.0 %middle.1 = (bf16[1,73,15,720]{3,2,1,0:T(8,128)(2,1)}, bf16[2,8,73,720]{3,2,1,0:T(8,128)(2,1)}, bf16[768,1920]{1,0:T(8,128)(2,1)}) custom-call(f32[16]{0:T(128)} %fusion.6.live_ref, f32[16]{0:T(128)} %get-tuple-element.21.area_ref, bf16[768,1920]{1,0:T(8,128)(2,1)} %bitcast.21, bf16[768,720]{1,0:T(8,128)(2,1)} %constant.76.clone.c_ref, ...), custom_call_target="tpu_custom_call" | custom-call | tf_op jit(solution)/shard_map/middle/pallas_call | solution.py:648
  185.2 0.0 copy-done.4
  185.2 0.6 pad_bitcast_fusion.enct_ref
  185.8 0.0 copy-done.5
  185.8 0.7 copy.25
  186.5 0.0 copy-start.2
  186.5 114.0 %backward.1 = bf16[1,73,15,720]{3,2,1,0:T(8,128)(2,1)} custom-call(f32[16]{0:T(128)} %get-tuple-element.20.weight_ref, f32[16]{0:T(128)} %fusion.6.live_ref, bf16[128,128]{1,0:T(8,128)(2,1)} %pad_bitcast_fusion.enct_ref, bf16[128,128]{1,0:T(8,128)(2,1)} %bitcast.23, f32[368,128]{1,0:T(8,128)} %gain_ref.3, bf16[73,128]{1,0:T(8,128)(2,1)} %enc_ref.1, ...), custom_call_target="tpu_custom_call" | custom-call | tf_op jit(solution)/shard_map/backward/pallas_call | solution.py:500
  300.5 0.0 copy-start
  300.5 0.0 copy-done.2
  300.5 1.2 copy.32
  301.8 0.9 copy-done
  302.7 1.2 copy.33
  (4 shorter events, 0.0 us)
Async XLA Ops:
  7.7 4.0 %copy-start.3 = (bf16[73,128]{0,1:T(8,128)(2,1)}, bf16[73,128]{0,1:T(8,128)(2,1)S(1)}, u32[]{:S(2)}) copy-start(bf16[73,128]{0,1:T(8,128)(2,1)S(1)} %copy.19) | copy-start | bytes 56068
  11.7 113.2 %copy-start.1 = (bf16[73,15,720]{2,1,0:T(8,128)(2,1)S(1)}, bf16[73,15,720]{2,1,0:T(8,128)(2,1)}, u32[]{:S(2)}) copy-start(bf16[73,15,720]{2,1,0:T(8,128)(2,1)} %param.10) | copy-start | bytes 4730404
  125.5 1.9 copy-start.6
  128.2 57.0 %copy-start.4 = (bf16[73,128]{0,1:T(8,128)(2,1)S(1)}, bf16[73,128]{0,1:T(8,128)(2,1)}, u32[]{:S(2)}) copy-start(bf16[73,128]{0,1:T(8,128)(2,1)} %copy-done.3) | copy-start | bytes 56068
  128.2 57.6 %copy-start.5 = (bf16[128,128]{1,0:T(8,128)(2,1)S(1)}, bf16[128,128]{1,0:T(8,128)(2,1)}, u32[]{:S(2)}) copy-start(bf16[128,128]{1,0:T(8,128)(2,1)} %mix_ref.1) | copy-start | bytes 98308
  186.5 114.0 %copy-start.2 = (bf16[1,73,15,720]{3,2,1,0:T(8,128)(2,1)S(1)}, bf16[1,73,15,720]{3,2,1,0:T(8,128)(2,1)}, u32[]{:S(2)}) copy-start(bf16[1,73,15,720]{3,2,1,0:T(8,128)(2,1)} %get-tuple-element.24) | copy-start | bytes 4730404
  300.5 2.1 copy-start

commit v6 on v5

--- a/solution.py
+++ b/solution.py
@@ -347,7 +347,8 @@
             gain = padded_gain(gain_ref) * order_factor(first_order + order)
             filtered = []
             for k in range(2):
-                channels = dot(coeffs[:, k * 128 : (k + 1) * 128], enc_ref[...], 1, 0).astype(BF16)
+                fields = coeffs[:, k * 128 : k * 128 + FIELDS]
+                channels = dot(fields, enc_ref[...], 1, 0).astype(BF16)
                 filtered.append((dot(channels, mix_ref[...], 1, 0) * gain).astype(BF16))
             scatter_points(dot(legt[m], jnp.concatenate(filtered, axis=1), 1, 0), made, order)
             return carry
@@ -373,7 +374,7 @@
 
 
 def backward_kernel(
-    weight_ref, live_ref, enct_ref, mixt_ref, gain_ref, enc_ref, dec_ref, c_ref, g_ref,
+    weight_ref, live_ref, enct_ref, mix_ref, gain_ref, enc_ref, dec_ref, c_ref, g_ref,
     leg_in, legt_in, z_ref, out_ref,
     leg, legt, arrived, rows, points, made, ready, sent_in, got_in, sent_out, got_out, kept,
     returned, spread, local, wide_rows, final, stored,
@@ -412,7 +413,7 @@
             back = []
             for k in range(2):
                 scaled = (grads[:, k * 128 : (k + 1) * 128] * gain).astype(BF16)
-                channels = dot(scaled, mixt_ref[...], 1, 0).astype(BF16)
+                channels = dot(scaled, mix_ref[...], 1, 1).astype(BF16)
                 back.append(dot(channels, enct_ref[...], 1, 0).astype(BF16))
             scatter_points(dot(legt[m], jnp.concatenate(back, axis=1), 1, 0), made, order)
             return carry
@@ -496,7 +497,7 @@
     )(weight, geo, diag, enc, mix, gain, c, x)
 
 
-def backward(weight, live, enct, mixt, gain, enc, dec, c, score, leg, legt, z):
+def backward(weight, live, enct, mix, gain, enc, dec, c, score, leg, legt, z):
     return pl.pallas_call(
         backward_kernel,
         in_specs=[SMEM] * 2 + [VMEM] * 7 + [ANY] * 2 + [VMEM],
@@ -513,7 +514,7 @@
         ],
         compiler_params=remote_params(2),
         name="backward",
-    )(weight, live, enct, mixt, gain, enc, dec, c, score, leg, legt, z)
+    )(weight, live, enct, mix, gain, enc, dec, c, score, leg, legt, z)
 
 
 def score_tile(p_ref, o_ref, out_ref, group, lanes, area):
@@ -705,7 +706,7 @@
 
     x = jnp.transpose(states[0], (1, 0, 2))
     synth, leg, legt = forward(
-        own_weight, geo, diag, enc_wide, mixing_weight, degree_gain, c, x
+        own_weight, geo, diag, enc, mixing_weight, degree_gain, c, x
     )
     synth = synth.reshape(BANDS * KM, WIDE)
     padded = jnp.pad(observed, ((0, 0), (0, 1), (0, 0)))
@@ -713,7 +714,7 @@
     prediction, score, grads = middle(own_live, own_area, synth, c, x, truth, enct, dect, dec)
 
     result = backward(
-        own_weight, own_live, enct_wide, mixing_weight.T, degree_gain, enc, dec, c, score,
+        own_weight, own_live, enct_wide, mixing_weight, degree_gain, enc, dec, c, score,
         leg, legt, grads.reshape(chunks(WIDE)),
     )
     return (prediction, result)

time: 304 us -> 302 us (level)
    unnamed x22 -> x18, local copies, waits for them, and re-layouts: 9.61 us -> 8.63 us
where the time goes in v6:
time: 302 us
  Pallas kernels  284 us (94%)
  local copies, waits for them, and re-layouts  12 us (4%)
  other arithmetic  5.12 us (2%)
    pallas_call x1, Pallas kernels, backward(): pl.pallas_call(backward_kernel, in_specs=[SMEM] * 2 + [VMEM] * 7 + [ANY]...  114 us
    pallas_call x1, Pallas kernels, forward(): pl.pallas_call(forward_kernel, in_specs=[SMEM] + [VMEM] * 7, out_specs=[V...  113 us
    pallas_call x1, Pallas kernels, middle(): pl.pallas_call(middle_kernel, in_specs=[SMEM] * 2 + [VMEM] * 7, out_specs...  56.9 us
    unnamed x18, local copies, waits for them, and re-layouts  8.63 us

profile of v6, /device:TPU:7, one launch (start us, length us, event | category | flops | bytes accessed | tf_op | source)
XLA Modules:
  0.0 302.0 jit_solution(11046119811981700434)
XLA Ops:
  0.6 1.3 fusion.5
  1.9 1.8 select_multiply_fusion
  3.8 0.7 dynamic-slice_bitcast_fusion
  4.5 0.7 broadcast.170.diag_ref
  5.1 0.7 select_reduce_fusion
  5.9 0.1 maximum_log_fusion
  6.0 0.6 stack.10.geo_ref
  6.6 3.3 %copy.24 = bf16[1,73,15,720]{3,1,2,0:T(8,128)(2,1)} copy(bf16[1,73,15,720]{3,2,1,0:T(8,128)(2,1)} %param.9) | data formatting | bytes 3153600 | tf_op args[0]
  9.9 0.0 copy-start.1
  9.9 113.3 %forward.1 = (bf16[3,32,8,1920]{3,2,1,0:T(8,128)(2,1)}, bf16[12,384,512]{2,1,0:T(8,128)(2,1)}, bf16[12,512,384]{2,1,0:T(8,128)(2,1)}) custom-call(f32[16]{0:T(128)} %get-tuple-element.20.weight_ref, f32[8,512]{1,0:T(8,128)} %stack.10.geo_ref, f32[16,128]{1,0:T(8,128)} %broadcast.170.diag_ref, bf16[73,128]{1,0:T(8,128)(2,1)} %enc_ref.3, ...), custom_call_target="tpu_custom_call" | custom-call | tf_op jit(solution)/shard_map/forward/pallas_call | solution.py:484
  123.2 0.0 copy-done.1
  123.2 0.5 copy.18
  123.8 0.0 copy-start.4
  123.8 0.0 copy-start.5
  123.8 0.7 fusion.o_ref
  124.6 1.1 fusion.6.live_ref
  125.7 0.0 copy-done.4
  125.7 0.7 copy.19
  126.4 0.0 copy-done.5
  126.4 0.7 copy.20.dec_ref
  127.1 0.0 copy-start.3
  127.2 56.9 %middle.1 = (bf16[1,73,15,720]{3,2,1,0:T(8,128)(2,1)}, bf16[2,8,73,720]{3,2,1,0:T(8,128)(2,1)}, bf16[768,1920]{1,0:T(8,128)(2,1)}) custom-call(f32[16]{0:T(128)} %fusion.6.live_ref, f32[16]{0:T(128)} %get-tuple-element.21.area_ref, bf16[768,1920]{1,0:T(8,128)(2,1)} %bitcast.20, bf16[768,720]{1,0:T(8,128)(2,1)} %constant.76.clone.c_ref, ...), custom_call_target="tpu_custom_call" | custom-call | tf_op jit(solution)/shard_map/middle/pallas_call | solution.py:649
  184.0 0.0 copy-done.3
  184.0 0.6 pad_bitcast_fusion.enct_ref
  184.7 0.0 copy-start.2
  184.7 114.0 %backward.1 = bf16[1,73,15,720]{3,2,1,0:T(8,128)(2,1)} custom-call(f32[16]{0:T(128)} %get-tuple-element.20.weight_ref, f32[16]{0:T(128)} %fusion.6.live_ref, bf16[128,128]{1,0:T(8,128)(2,1)} %pad_bitcast_fusion.enct_ref, bf16[128,128]{1,0:T(8,128)(2,1)} %mix_ref.3, f32[368,128]{1,0:T(8,128)} %gain_ref.3, bf16[73,128]{1,0:T(8,128)(2,1)} %enc_ref.3, ...), custom_call_target="tpu_custom_call" | custom-call | tf_op jit(solution)/shard_map/backward/pallas_call | solution.py:501
  298.6 0.0 copy-start
  298.7 0.0 copy-done.2
  298.7 1.2 copy.27
  299.9 0.9 copy-done
  300.8 1.2 copy.28
  (4 shorter events, 0.0 us)
Async XLA Ops:
  9.9 113.3 %copy-start.1 = (bf16[73,15,720]{2,1,0:T(8,128)(2,1)S(1)}, bf16[73,15,720]{2,1,0:T(8,128)(2,1)}, u32[]{:S(2)}) copy-start(bf16[73,15,720]{2,1,0:T(8,128)(2,1)} %param.10) | copy-start | bytes 4730404
  123.8 1.9 copy-start.4
  123.8 2.6 copy-start.5
  127.1 56.9 %copy-start.3 = (bf16[73,128]{0,1:T(8,128)(2,1)S(1)}, bf16[73,128]{0,1:T(8,128)(2,1)}, u32[]{:S(2)}) copy-start(bf16[73,128]{0,1:T(8,128)(2,1)} %copy.19) | copy-start | bytes 56068
  184.7 114.0 %copy-start.2 = (bf16[1,73,15,720]{3,2,1,0:T(8,128)(2,1)S(1)}, bf16[1,73,15,720]{3,2,1,0:T(8,128)(2,1)}, u32[]{:S(2)}) copy-start(bf16[1,73,15,720]{3,2,1,0:T(8,128)(2,1)} %get-tuple-element.24) | copy-start | bytes 4730404
  298.6 2.1 copy-start
